TPU v7x, 32 devices: a whole 2x2x4 slice. The times are simulated.
32 devices in a mesh: dom: 8 (over z, y), sub: 4 (over x, core).
Axes of the slice: x: 2, y: 2, z: 4, core: 2. Of those that a mesh axis runs over, the one named last changes fastest.
Arguments:
- node_state: bfloat16 [64, 32768], P(None, ('dom', 'sub')), may hold values from -6 to 6
- edge_state: bfloat16 [64, 98304], P(None, ('dom', 'sub')), may hold values from -6 to 6
- senders: int32 [98304], P(('dom', 'sub')), may hold values from 0 to 2559, as said below
- receivers: int32 [98304], P(('dom', 'sub')), may hold values from 0 to 1023
- send_index: int32 [32, 12, 128], P(('dom', 'sub')), may hold values from -1 to 1023, as said below
- node_cotangent: bfloat16 [64, 32768], P(None, ('dom', 'sub')), may hold values from -6 to 6
- edge_cotangent: bfloat16 [64, 98304], P(None, ('dom', 'sub')), may hold values from -6 to 6
- edge_first: bfloat16 [192, 64], replicated, may hold values from -0.4375 to 0.4375
- edge_bias: float32 [64], replicated, may hold values from -3 to 3
- edge_second: bfloat16 [64, 64], replicated, may hold values from -0.75 to 0.75
- edge_gain: float32 [64], replicated, may hold values from 0.1 to 1.9
- edge_shift: float32 [64], replicated, may hold values from -3 to 3
- node_first: bfloat16 [128, 64], replicated, may hold values from -0.5 to 0.5
- node_bias: float32 [64], replicated, may hold values from -3 to 3
- node_second: bfloat16 [64, 64], replicated, may hold values from -0.75 to 0.75
- node_gain: float32 [64], replicated, may hold values from 0.1 to 1.9
Outputs:
- delta_state: bfloat16 [64, 32768], P(None, ('dom', 'sub'))
- delta_edges: bfloat16 [64, 98304], P(None, ('dom', 'sub'))
- delta_edgefirst: float32 [192, 64], replicated
- delta_edgebias: float32 [64], replicated
- delta_edgesecond: float32 [64, 64], replicated
- delta_edgegain: float32 [64], replicated
- delta_edgeshift: float32 [64], replicated
- delta_nodefirst: float32 [128, 64], replicated
- delta_nodebias: float32 [64], replicated
- delta_nodesecond: float32 [64, 64], replicated
- delta_nodegain: float32 [64], replicated
- delta_nodeshift: float32 [64], replicated
Inputs may be any that keep to these rules, and one draw needn't show every extreme that they name: `send_index`: block k = o * 4 + t of partition p = d * 4 + s lists own cells that p sends to the partition at dom index d + o - 1 and sub index t: live entries first, then -1. Blocks towards a dom index outside the mesh, and block 4 + s, hold only -1; every other block holds 32 to 128 live entries. Some partition receives a full block from every partition that sends to it. `senders`: an entry below 1024 is an own cell. An entry 1024 + k * 128 + j with k = o * 4 + u names ghost slot j of block k: the j-th entry of block o * 4 + s of the partition at dom index d + 1 - o and sub index u, and that entry is live.
All inputs are finite; a program needn't handle non-finite values.
Results may differ from a plain program's by a relative error of at most 0.0095.
Values may be sent and summed in bfloat16 or wider, within the bound.
A program may use at most 64 MiB of HBM per device.

v0:
```python
import functools
import math

import jax
import jax.numpy as jnp
from jax import lax
from jax.experimental import pallas as pl
from jax.experimental.pallas import tpu as pltpu
from jax.sharding import PartitionSpec as P

EPSILON = 1e-05
MESH = pl.DeviceIdType.MESH
BF = jnp.bfloat16
F32 = jnp.float32


def nn(a, b):
    return lax.dot_general(a, b, (((1,), (0,)), ((), ())), preferred_element_type=F32)


def nt(a, b):
    return lax.dot_general(a, b, (((1,), (1,)), ((), ())), preferred_element_type=F32)


def flip(a):
    return a.astype(F32).T


def one_hot(index, rows):
    return jnp.where(lax.broadcasted_iota(jnp.int32, (rows, index.shape[1]), 0) == index, 1.0, 0.0).astype(BF)


def standardize(values):
    centered = values - jnp.mean(values, axis=0, keepdims=True)
    spread = lax.rsqrt(jnp.mean(centered * centered, axis=0, keepdims=True) + EPSILON)
    return centered * spread, spread


def normalize_back(upstream, scaled, spread, gain):
    weighted = upstream * gain
    return spread * (
        weighted
        - jnp.mean(weighted, axis=0, keepdims=True)
        - scaled * jnp.mean(weighted * scaled, axis=0, keepdims=True)
    )


def packed_rows(features):
    half = 3 * features // 2
    return half, half + features, half + 2 * features


def fold_lanes(values):
    total = values[:, :128]
    for begin in range(128, values.shape[1], 128):
        total = total + values[:, begin : begin + 128]
    return total


def halo_peers(dom, sub):
    d, s = lax.axis_index("dom"), lax.axis_index("sub")
    for o in (0, 2, 1):
        for r in range(sub):
            if o == 1 and r == 0:
                continue
            t = lax.rem(s + r, sub)
            target = d + (o - 1)
            yield o, t, target, (target >= 0) & (target < dom)


def halo_copy(outgoing, incoming, send_sem, recv_sem, source, landing, target, t):
    return pltpu.make_async_remote_copy(
        src_ref=outgoing.at[source],
        dst_ref=incoming.at[landing],
        send_sem=send_sem.at[source],
        recv_sem=recv_sem.at[landing],
        device_id=(target, t),
        device_id_type=MESH,
    )


def guarded(o, there, action):
    if o == 1:
        action()
    else:
        pl.when(there)(action)


def start_exchange(dom, sub, s, outgoing, incoming, send_sem, recv_sem, forward):
    for o, t, target, there in halo_peers(dom, sub):
        block = o if forward else 2 - o

        def start(block=block, t=t, target=target):
            halo_copy(outgoing, incoming, send_sem, recv_sem, block * sub + t, block * sub + s, target, t).start()

        guarded(o, there, start)
    d = lax.axis_index("dom")
    incoming[sub + s] = jnp.zeros(incoming.shape[1:], incoming.dtype)
    for o in (0, 2):
        origin = d + 1 - o if forward else d + o - 1

        @pl.when((origin < 0) | (origin >= dom))
        def _():
            for u in range(sub):
                incoming[o * sub + u] = jnp.zeros(incoming.shape[1:], incoming.dtype)


def finish_exchange(dom, sub, s, outgoing, incoming, send_sem, recv_sem, forward):
    for o, t, target, there in halo_peers(dom, sub):
        block = 2 - o if forward else o

        def finish(block=block, t=t, target=target):
            halo_copy(outgoing, incoming, send_sem, recv_sem, block * sub + t, block * sub + t, target, t).wait_recv()

        guarded(o, there, finish)
    for o, t, target, there in halo_peers(dom, sub):
        block = o if forward else 2 - o

        def finish(block=block, t=t, target=target):
            halo_copy(outgoing, incoming, send_sem, recv_sem, block * sub + t, block * sub + t, target, t).wait_send()

        guarded(o, there, finish)


def layer_kernel(
    dom, sub, chunk,
    node_ref, edge_ref, senders_ref, receivers_ref, index_ref, node_cot_ref, edge_cot_ref,
    edge_first_ref, edge_second_ref, node_first_ref, node_second_ref,
    edge_bias_ref, edge_gain_ref, edge_shift_ref, node_bias_ref, node_gain_ref,
    state_ref, edge_out_ref, sum_ref,
    outgoing, incoming, returning, returned, exports,
    selector, extended, slope, active, scaled_all, spread_all, summed, sums, small, lanes, local,
    packed_ref, pieces, reduced,
    send_sem, recv_sem, back_send, back_recv, part_send, part_recv, whole_send, whole_recv,
):
    features, cells = node_ref.shape
    faces = edge_ref.shape[1]
    peers, _, halo = outgoing.shape
    width = extended.shape[1]
    step = 128
    d, s = lax.axis_index("dom"), lax.axis_index("sub")
    count = dom * sub
    me = d * sub + s
    rows = reduced.shape[0]
    barrier = pltpu.get_barrier_semaphore()

    def place(r):
        other = lax.rem(me + r, count)
        return other, (other // sub, lax.rem(other, sub))

    def greet(r, carry):
        _, device = place(r)
        pl.semaphore_signal(barrier, inc=1, device_id=device, device_id_type=MESH)
        return carry

    lax.fori_loop(1, count, greet, 0)

    def pick(number, carry):
        chosen = index_ref[:, pl.ds(pl.multiple_of(number * 2 * halo, 2 * halo), 2 * halo)]
        exports[number] = one_hot(chosen, cells)
        picked = nn(node_ref[...], exports[number]).astype(BF)
        outgoing[2 * number] = picked[:, :halo]
        outgoing[2 * number + 1] = picked[:, halo:]
        return carry

    lax.fori_loop(0, peers // 2, pick, 0)
    pl.semaphore_wait(barrier, count - 1)
    start_exchange(dom, sub, s, outgoing, incoming, send_sem, recv_sem, forward=True)

    edge_first_t = edge_first_ref[...]
    edge_first = flip(edge_first_t).astype(BF)
    edge_second = edge_second_ref[...]
    edge_second_t = flip(edge_second).astype(BF)
    vectors = [edge_bias_ref, edge_gain_ref, edge_shift_ref, node_bias_ref, node_gain_ref]
    table = jnp.concatenate([v[...] for v in vectors] + [jnp.zeros((3, features), F32)], axis=0).T
    edge_bias, edge_gain, edge_shift, node_bias, node_gain = (table[:, i : i + 1] for i in range(5))
    summed[...] = jnp.zeros(summed.shape, F32)
    row = lax.broadcasted_iota(jnp.int32, (step, chunk), 0)
    one, zero = jnp.ones((step, chunk), BF), jnp.zeros((step, chunk), BF)

    def prepare(c, carry):
        here = pl.ds(pl.multiple_of(c * chunk, chunk), chunk)
        sender = senders_ref[:, here]
        receiver = receivers_ref[:, here]

        def fill(begin, index):
            offset = (jnp.broadcast_to(index, (step, chunk)) - row).astype(jnp.int16)

            def body(i, inner):
                at = pl.multiple_of(i * step, step)
                hit = offset == jnp.full((step, chunk), at, jnp.int32).astype(jnp.int16)
                selector[c, pl.ds(pl.multiple_of(begin + at, step), step), :] = jnp.where(hit, one, zero)
                return inner
            return body

        lax.fori_loop(0, width // step, fill(0, sender), 0)
        lax.fori_loop(0, cells // step, fill(width, receiver), 0)
        received = nn(node_ref[...], selector[c, width:, :]).astype(BF)
        stacked = jnp.concatenate([received, edge_ref[:, here]], axis=0)
        slope[:, here] = nn(edge_first_t[:, features:], stacked) + edge_bias
        return carry

    lax.fori_loop(0, faces // chunk, prepare, 0)
    finish_exchange(dom, sub, s, outgoing, incoming, send_sem, recv_sem, forward=True)
    extended[:, :cells] = node_ref[...]
    for k in range(peers):
        extended[:, cells + k * halo : cells + (k + 1) * halo] = incoming[k]

    def forward(c, carry):
        here = pl.ds(pl.multiple_of(c * chunk, chunk), chunk)
        sent = nn(extended[...], selector[c, :width, :]).astype(BF)
        linear = nn(edge_first_t[:, :features], sent) + slope[:, here]
        logistic = jax.nn.sigmoid(linear)
        lively = (linear * logistic).astype(BF)
        slope[:, here] = logistic * (1.0 + linear * (1.0 - logistic))
        active[:, here] = lively
        scaled, spread = standardize(nn(edge_second_t, lively))
        scaled_all[:, here] = scaled
        spread_all[:, here] = spread
        message = (scaled * edge_gain + edge_shift).astype(BF)
        summed[...] += nt(selector[c, width:, :], message)
        return carry

    lax.fori_loop(0, faces // chunk, forward, 0)

    node_first_t = node_first_ref[...]
    node_first = flip(node_first_t).astype(BF)
    node_second_t = flip(node_second_ref[...]).astype(BF)
    node_input = jnp.concatenate([node_ref[...], summed[...].T.astype(BF)], axis=0)
    node_linear = nn(node_first_t, node_input) + node_bias
    node_logistic = jax.nn.sigmoid(node_linear)
    node_active = (node_linear * node_logistic).astype(BF)
    node_scaled, node_spread = standardize(nn(node_second_t, node_active))
    upstream = node_cot_ref[...].astype(F32)
    lanes[3] = fold_lanes(upstream * node_scaled)
    lanes[4] = fold_lanes(upstream)
    node_delta = normalize_back(upstream, node_scaled, node_spread, node_gain).astype(BF)
    node_slope = node_logistic * (1.0 + node_linear * (1.0 - node_logistic))
    node_hidden = nn(node_second_ref[...], node_delta) * node_slope
    lanes[5] = fold_lanes(node_hidden)
    node_hidden = node_hidden.astype(BF)
    node_first_delta = nt(node_input, node_hidden)
    half, mid, top = packed_rows(features)
    packed_ref[half:mid, :features] = node_first_delta[:features]
    packed_ref[half:mid, features:] = node_first_delta[features:]
    packed_ref[mid:top, features:] = nt(node_active, node_delta)
    node_back = nn(node_first, node_hidden)
    local[...] = node_back[:features] + upstream
    toward = node_back[features:]
    high = toward.astype(BF)
    low = (toward - high.astype(F32)).astype(BF)
    toward = jnp.concatenate([high, low], axis=0)

    small[...] = jnp.zeros(small.shape, F32)
    for i in range(3):
        lanes[i] = jnp.zeros(lanes.shape[1:], F32)

    def backward(c, carry):
        here = pl.ds(pl.multiple_of(c * chunk, chunk), chunk)
        gathered = nn(toward, selector[c, width:, :])
        cotangent = edge_cot_ref[:, here].astype(F32)
        delta = cotangent + (gathered[:features] + gathered[features:])
        scaled = scaled_all[:, here]
        lanes[0] += fold_lanes(delta * scaled)
        lanes[1] += fold_lanes(delta)
        edge_delta = normalize_back(delta, scaled, spread_all[:, here], edge_gain).astype(BF)
        small[0] += nt(active[:, here], edge_delta)
        hidden = nn(edge_second, edge_delta) * slope[:, here]
        lanes[2] += fold_lanes(hidden)
        hidden = hidden.astype(BF)
        active[:, here] = hidden
        small[1] += nt(edge_ref[:, here], hidden)
        return carry

    lax.fori_loop(0, faces // chunk, backward, 0)
    block = math.gcd(width + cells, 512)

    def gather_sums(i, carry):
        at = pl.ds(pl.multiple_of(i * block, block), block)
        total = nt(selector[0, at, :], active[:, :chunk])
        for c in range(1, faces // chunk):
            total = total + nt(selector[c, at, :], active[:, c * chunk : (c + 1) * chunk])
        sums[at, :] = total
        return carry

    lax.fori_loop(0, (width + cells) // block, gather_sums, 0)

    by_sender = sums[:width, :].astype(BF)
    by_receiver = sums[width:, :].astype(BF)
    back = nt(edge_first[:features], by_sender)
    for k in range(peers):
        returning[k] = back[:, cells + k * halo : cells + (k + 1) * halo].astype(BF)
    first = nn(extended[...], by_sender)
    second = nn(node_ref[...], by_receiver)
    packed_ref[0:features, :features] = first
    packed_ref[features:half, :features] = second[: half - features]
    packed_ref[0 : 2 * features - half, features:] = second[half - features :]
    packed_ref[2 * features - half : half, features:] = small[1]
    packed_ref[mid:top, :features] = small[0]
    column = lax.broadcasted_iota(jnp.int32, (features, 128), 1)
    vectors = jnp.zeros((features, 128), F32)
    for i in range(6):
        vectors = jnp.where(column == i, jnp.sum(lanes[i], axis=1, keepdims=True), vectors)
    packed_ref[top:, :] = jnp.zeros((packed_ref.shape[0] - top, 128), F32)
    packed_ref[top : top + 8, :features] = vectors.T[:8]

    def part_copy(source, landing, device):
        return pltpu.make_async_remote_copy(
            src_ref=packed_ref.at[pl.ds(pl.multiple_of(source * rows, 8), rows)],
            dst_ref=pieces.at[landing],
            send_sem=part_send.at[source],
            recv_sem=part_recv.at[landing],
            device_id=device,
            device_id_type=MESH,
        )

    def whole_copy(landing, device, other):
        return pltpu.make_async_remote_copy(
            src_ref=reduced,
            dst_ref=sum_ref.at[pl.ds(pl.multiple_of(landing * rows, 8), rows)],
            send_sem=whole_send.at[other],
            recv_sem=whole_recv.at[landing],
            device_id=device,
            device_id_type=MESH,
        )

    def send_part(r, carry):
        other, device = place(r)
        part_copy(other, me, device).start()
        return carry

    lax.fori_loop(1, count, send_part, 0)
    start_exchange(dom, sub, s, returning, returned, back_send, back_recv, forward=False)
    local[...] += back[:, :cells] + nt(edge_first[features : 2 * features], by_receiver)

    def emit(c, carry):
        here = pl.ds(pl.multiple_of(c * chunk, chunk), chunk)
        ahead = nn(edge_first[2 * features :], active[:, here])
        edge_out_ref[:, here] = (edge_cot_ref[:, here].astype(F32) + ahead).astype(BF)
        return carry

    lax.fori_loop(0, faces // chunk, emit, 0)
    own = pl.ds(pl.multiple_of(me * rows, 8), rows)

    def take_part(r, total):
        other, device = place(r)
        part_copy(other, other, device).wait_recv()
        return total + pieces[other]

    reduced[...] = lax.fori_loop(1, count, take_part, packed_ref[own, :])

    def send_whole(r, carry):
        other, device = place(r)
        whole_copy(me, device, other).start()
        return carry

    lax.fori_loop(1, count, send_whole, 0)
    sum_ref[own, :] = reduced[...]
    finish_exchange(dom, sub, s, returning, returned, back_send, back_recv, forward=False)
    summed[...] = jnp.zeros(summed.shape, F32)

    def scatter(i, carry):
        value = jnp.concatenate([returned[2 * i], returned[2 * i + 1]], axis=1)
        summed[...] += nt(exports[i], value)
        return carry

    lax.fori_loop(0, peers // 2, scatter, 0)
    state_ref[...] = (local[...] + summed[...].T).astype(BF)

    def settle(r, carry):
        other, device = place(r)
        part_copy(other, other, device).wait_send()
        whole_copy(other, device, other).wait_send()
        whole_copy(other, device, other).wait_recv()
        return carry

    lax.fori_loop(1, count, settle, 0)


def unpack_kernel(
    factor, state_in, edge_in, sum_ref,
    state_ref, edge_ref, edge_first_ref, edge_second_ref, node_first_ref, node_second_ref, *vector_refs,
):
    features = state_in.shape[0]
    half, mid, top = packed_rows(features)
    state_ref[...] = state_in[...]
    edge_ref[...] = edge_in[...]
    left = sum_ref[:, :features] * factor
    right = sum_ref[:, features:] * factor
    edge_first_ref[...] = jnp.concatenate([left[:half], right[:half]], axis=0).T
    node_first_ref[...] = jnp.concatenate([left[half:mid], right[half:mid]], axis=0).T
    edge_second_ref[...] = left[mid:top]
    node_second_ref[...] = right[mid:top]
    for i, vector_ref in enumerate(vector_refs):
        vector_ref[...] = left[top + i : top + i + 1]


def on_device(
    dom, sub,
    node_state, edge_state, senders, receivers, send_index, node_cotangent, edge_cotangent,
    edge_first, edge_bias, edge_second, edge_gain, edge_shift, node_first, node_bias, node_second, node_gain,
):
    features, cells = node_state.shape
    faces = edge_state.shape[1]
    halo = send_index.shape[2]
    peers = 3 * sub
    ghosts = peers * halo
    width = cells + ghosts
    count = dom * sub
    rows = -(-(packed_rows(features)[2] + 8) // (8 * count)) * 8
    chunk = math.gcd(faces, 512)
    vmem = pl.BlockSpec(memory_space=pltpu.VMEM)
    shape = jax.ShapeDtypeStruct
    dma = pltpu.SemaphoreType.DMA

    def line(vector):
        return vector.reshape(1, -1)

    state, edge_result, total = pl.pallas_call(
        functools.partial(layer_kernel, dom, sub, chunk),
        out_shape=(
            shape((features, cells), BF),
            shape((features, faces), BF),
            shape((count * rows, 128), F32),
        ),
        in_specs=[vmem] * 16,
        out_specs=(vmem,) * 3,
        scratch_shapes=[pltpu.VMEM((peers, features, halo), BF)] * 4
        + [
            pltpu.VMEM((peers // 2, cells, 2 * halo), BF),
            pltpu.VMEM((faces // chunk, width + cells, chunk), BF),
            pltpu.VMEM((features, width), BF),
            pltpu.VMEM((features, faces), F32),
            pltpu.VMEM((features, faces), BF),
            pltpu.VMEM((features, faces), F32),
            pltpu.VMEM((1, faces), F32),
            pltpu.VMEM((cells, features), F32),
            pltpu.VMEM((width + cells, features), F32),
            pltpu.VMEM((2, features, features), F32),
            pltpu.VMEM((6, features, 128), F32),
            pltpu.VMEM((features, cells), F32),
            pltpu.VMEM((count * rows, 128), F32),
            pltpu.VMEM((count, rows, 128), F32),
            pltpu.VMEM((rows, 128), F32),
        ]
        + [dma((peers,))] * 4
        + [dma((count,))] * 4,
        compiler_params=pltpu.CompilerParams(
            collective_id=0, has_side_effects=True, vmem_limit_bytes=60 * 1024 * 1024
        ),
        name="layer",
    )(
        node_state, edge_state, line(senders), line(receivers), line(send_index),
        node_cotangent, edge_cotangent, edge_first.T, edge_second, node_first.T, node_second,
        line(edge_bias), line(edge_gain), line(edge_shift), line(node_bias), line(node_gain),
    )
    vector = shape((1, features), F32)
    state, edge_result, edge_first_sum, edge_second_sum, node_first_sum, node_second_sum, *vectors = pl.pallas_call(
        functools.partial(unpack_kernel, 1.0 / math.sqrt(faces * count)),
        out_shape=(
            shape((features, cells), BF),
            shape((features, faces), BF),
            shape(edge_first.shape[::-1], F32),
            shape(edge_second.shape, F32),
            shape(node_first.shape[::-1], F32),
            shape(node_second.shape, F32),
        )
        + (vector,) * 6,
        in_specs=[vmem] * 3,
        out_specs=(vmem,) * 12,
        name="unpack",
    )(state, edge_result, total)
    vectors = [v.reshape(-1) for v in vectors]
    return (
        state, edge_result, edge_first_sum.T, vectors[2], edge_second_sum, vectors[0], vectors[1],
        node_first_sum.T, vectors[5], node_second_sum, vectors[3], vectors[4],
    )


def solution(mesh):
    split = P(None, ("dom", "sub"))
    faces = P(("dom", "sub"))
    return jax.shard_map(
        functools.partial(on_device, mesh.shape["dom"], mesh.shape["sub"]),
        mesh=mesh,
        in_specs=(split, split, faces, faces, P(("dom", "sub"), None, None), split, split) + (P(),) * 9,
        out_specs=(split, split) + (P(),) * 10,
        check_vma=False,
    )
```

profile of v0, /device:TPU:0, one launch (start us, length us, event | category | flops | bytes accessed | tf_op | source)
XLA Modules:
  0.0 51.5 jit_solution(3085338478857963652)
XLA Ops:
  0.7 48.8 %layer.1 = (bf16[64,1024]{1,0:T(8,128)(2,1)}, bf16[64,3072]{1,0:T(8,128)(2,1)}, f32[256,128]{1,0:T(8,128)}) custom-call(bf16[64,1024]{1,0:T(8,128)(2,1)} %node_ref.1, bf16[64,3072]{1,0:T(8,128)(2,1)} %edge_ref.1, s32[1,3072]{1,0:T(1,128)} %bitcast.20, s32[1,3072]{1,0:T(1,128)} %bitcast.21, s32[1,1536]{1,0:T(1,128)} %bitcast.22, ...), custom_call_target="tpu_custom_call" | custom-call | tf_op jit(solution)/shard_map/layer/pallas_call | solution.py:419
  49.4 2.1 %unpack.1 = (bf16[64,1024]{1,0:T(8,128)(2,1)}, bf16[64,3072]{1,0:T(8,128)(2,1)}, f32[64,192]{1,0:T(8,128)}, f32[64,64]{1,0:T(8,128)}, f32[64,128]{1,0:T(8,128)},...) custom-call(bf16[64,1024]{1,0:T(8,128)(2,1)} %get-tuple-element.27.s, ...), custom_call_target="tpu_custom_call" | custom-call | tf_op jit(solution)/shard_map/unpack/pallas_call | solution.py:458
where the time goes:
time: 51.7 us; the launch traced here: 51.5 us
  Pallas kernels  50.9 us (98%)
  between operations  0.66 us (1%)
    pallas_call x1, Pallas kernels, on_device(): pl.pallas_call(functools.partial(layer_kernel, dom, sub, chunk), out_shap...  48.8 us
    pallas_call x1, Pallas kernels, on_device(): pl.pallas_call(functools.partial(unpack_kernel, 1.0 / math.sqrt(faces * c...  2.09 us

commit v1 on v0

v1 whole, which is shorter than its diff:
```python
import functools
import math

import jax
import jax.numpy as jnp
from jax import lax
from jax.experimental import pallas as pl
from jax.experimental.pallas import tpu as pltpu
from jax.sharding import PartitionSpec as P

EPSILON = 1e-05
MESH = pl.DeviceIdType.MESH
BF = jnp.bfloat16
F32 = jnp.float32
LOW = 256
PIECE = 8


def nn(a, b):
    return lax.dot_general(a, b, (((1,), (0,)), ((), ())), preferred_element_type=F32)


def nt(a, b):
    return lax.dot_general(a, b, (((1,), (1,)), ((), ())), preferred_element_type=F32)


def flip(a):
    return a.astype(F32).T


def standardize(values):
    centered = values - jnp.mean(values, axis=0, keepdims=True)
    spread = lax.rsqrt(jnp.mean(centered * centered, axis=0, keepdims=True) + EPSILON)
    return centered * spread, spread


def normalize_back(upstream, scaled, spread, gain):
    weighted = upstream * gain
    return spread * (
        weighted
        - jnp.mean(weighted, axis=0, keepdims=True)
        - scaled * jnp.mean(weighted * scaled, axis=0, keepdims=True)
    )


def lively_and_slope(linear):
    half = 0.5 * linear
    tilt = jnp.tanh(half)
    logistic = 0.5 + 0.5 * tilt
    lively = half + half * tilt
    return lively, logistic + lively * (1.0 - logistic)


def fold_lanes(values):
    total = values[:, :128]
    for begin in range(128, values.shape[1], 128):
        total = total + values[:, begin : begin + 128]
    return total


def stack_blocks(table):
    return jnp.concatenate([table[:, i : i + LOW] for i in range(0, table.shape[1], LOW)], axis=0)


def write_selector(selector, at, index):
    width = index.shape[1]
    low = jnp.bitwise_and(index, LOW - 1)
    offset = jnp.broadcast_to(low, (16, width)) - lax.broadcasted_iota(jnp.int32, (16, width), 0)
    offset = offset.astype(F32).astype(BF)
    one, zero = jnp.ones((16, width), BF), jnp.zeros((16, width), BF)
    for begin in range(0, LOW, 16):
        selector[begin : begin + 16, at] = jnp.where(offset == jnp.asarray(begin, BF), one, zero)


def choose(stacked, high, first, base):
    features = base.shape[0]
    high = jnp.broadcast_to(high, base.shape)
    for i in range(stacked.shape[0] // features):
        base = jnp.where(high == first + i, stacked[i * features : (i + 1) * features], base)
    return base


def spread_blocks(values, high, blocks):
    high = jnp.concatenate([high] * (values.shape[0] // 16), axis=0)
    zero = jnp.zeros(values.shape, values.dtype)
    return jnp.concatenate([jnp.where(high == jnp.asarray(i, BF), values, zero) for i in blocks], axis=0)


def high_part(index):
    return jnp.right_shift(index, 8)


def high_rows(index):
    return jnp.broadcast_to(high_part(index), (16, index.shape[1])).astype(F32).astype(BF)


def halo_peers(dom, sub):
    d, s = lax.axis_index("dom"), lax.axis_index("sub")
    for o in (0, 2, 1):
        for r in range(sub):
            if o == 1 and r == 0:
                continue
            t = lax.rem(s + r, sub)
            target = d + (o - 1)
            yield o, t, target, (target >= 0) & (target < dom)


def halo_copy(outgoing, incoming, send_sem, recv_sem, source, landing, target, t):
    return pltpu.make_async_remote_copy(
        src_ref=outgoing.at[source],
        dst_ref=incoming.at[landing],
        send_sem=send_sem.at[source],
        recv_sem=recv_sem.at[landing],
        device_id=(target, t),
        device_id_type=MESH,
    )


def guarded(o, there, action):
    if o == 1:
        action()
    else:
        pl.when(there)(action)


def start_exchange(dom, sub, s, outgoing, incoming, send_sem, recv_sem, forward):
    for o, t, target, there in halo_peers(dom, sub):
        block = o if forward else 2 - o

        def start(block=block, t=t, target=target):
            halo_copy(outgoing, incoming, send_sem, recv_sem, block * sub + t, block * sub + s, target, t).start()

        guarded(o, there, start)


def clear_absent(dom, sub, s, incoming, forward):
    d = lax.axis_index("dom")
    incoming[sub + s] = jnp.zeros(incoming.shape[1:], incoming.dtype)
    for o in (0, 2):
        origin = d + 1 - o if forward else d + o - 1

        @pl.when((origin < 0) | (origin >= dom))
        def _():
            for u in range(sub):
                incoming[o * sub + u] = jnp.zeros(incoming.shape[1:], incoming.dtype)


def finish_exchange(dom, sub, s, outgoing, incoming, send_sem, recv_sem, forward):
    for o, t, target, there in halo_peers(dom, sub):
        block = 2 - o if forward else o

        def finish(block=block, t=t, target=target):
            halo_copy(outgoing, incoming, send_sem, recv_sem, block * sub + t, block * sub + t, target, t).wait_recv()

        guarded(o, there, finish)


def settle_exchange(dom, sub, s, outgoing, incoming, send_sem, recv_sem, forward):
    for o, t, target, there in halo_peers(dom, sub):
        block = o if forward else 2 - o

        def finish(block=block, t=t, target=target):
            halo_copy(outgoing, incoming, send_sem, recv_sem, block * sub + t, block * sub + t, target, t).wait_send()

        guarded(o, there, finish)


def edge_owner(count, j):
    return count // 2 - 8 + j


def node_owner(count, j):
    return j + jnp.where(j < 8, 0, count - 16) if not isinstance(j, int) else (j if j < 8 else count - 16 + j)


class Reduction:
    def __init__(self, count, sub, me, number, owner, owned, packed, landing, reduced, result, sems):
        self.count, self.sub, self.me = count, sub, me
        self.number, self.owner, self.owned = number, owner, owned
        self.packed, self.landing, self.reduced, self.result = packed, landing, reduced, result
        self.part_send, self.part_recv, self.whole_send, self.whole_recv = sems
        self.is_owner, self.mine = owned

    def device(self, rank):
        return (rank // self.sub, lax.rem(rank, self.sub))

    def part(self, j, source, rank):
        return pltpu.make_async_remote_copy(
            src_ref=self.packed.at[j],
            dst_ref=self.landing.at[source],
            send_sem=self.part_send.at[j],
            recv_sem=self.part_recv.at[source],
            device_id=self.device(rank),
            device_id_type=MESH,
        )

    def whole(self, j, rank):
        return pltpu.make_async_remote_copy(
            src_ref=self.reduced,
            dst_ref=self.result.at[j],
            send_sem=self.whole_send.at[rank],
            recv_sem=self.whole_recv.at[j],
            device_id=self.device(rank),
            device_id_type=MESH,
        )

    def send_parts(self):
        def body(j, carry):
            rank = self.owner(self.count, j)

            @pl.when(rank != self.me)
            def _():
                self.part(j, self.me, rank).start()

            return carry

        lax.fori_loop(0, self.number, body, 0)

    def others(self, action):
        def body(r, carry):
            rank = lax.rem(self.me + r, self.count)
            action(rank)
            return carry

        lax.fori_loop(1, self.count, body, 0)

    def reduce(self):
        @pl.when(self.is_owner)
        def _():
            def take(r, total):
                rank = lax.rem(self.me + r, self.count)
                self.part(self.mine, rank, rank).wait_recv()
                return total + self.landing[rank].astype(F32)

            total = lax.fori_loop(1, self.count, take, self.packed[self.mine].astype(F32))
            self.reduced[...] = total.astype(BF)
            self.result[self.mine] = total.astype(BF)
            self.others(lambda rank: self.whole(self.mine, rank).start())

    def settle(self):
        def body(j, carry):
            rank = self.owner(self.count, j)

            @pl.when(rank != self.me)
            def _():
                self.part(j, rank, rank).wait_send()
                self.whole(j, rank).wait_recv()

            return carry

        lax.fori_loop(0, self.number, body, 0)

        @pl.when(self.is_owner)
        def _():
            self.others(lambda rank: self.whole(self.mine, rank).wait_send())


def layer_kernel(
    dom, sub, chunk,
    node_in, edge_in, senders_in, receivers_in, index_in, node_cot_in, edge_cot_in,
    edge_first_in, edge_second_in, node_first_in, node_second_in,
    edge_bias_in, edge_gain_in, edge_shift_in, node_bias_in, node_gain_in,
    state_ref, edge_out_ref, edge_sum, node_sum,
    node_ref, edge_ref, senders_ref, receivers_ref, index_ref, node_cot_ref, edge_cot_ref,
    edge_first_ref, edge_second_ref, node_first_ref, node_second_ref,
    edge_bias_ref, edge_gain_ref, edge_shift_ref, node_bias_ref, node_gain_ref,
    outgoing, incoming, returning, returned,
    export_sel, sender_sel, receiver_sel, sender_high, receiver_high, export_high,
    stacked, slope, active, scaled_all, spread_all, summed, by_sender, by_receiver, grads, lanes, local,
    edge_packed, node_packed, edge_landing, node_landing, edge_reduced, node_reduced,
    load_sem, send_sem, recv_sem, back_send, back_recv,
    edge_part_send, edge_part_recv, edge_whole_send, edge_whole_recv,
    node_part_send, node_part_recv, node_whole_send, node_whole_recv,
):
    features, cells = node_ref.shape
    faces = edge_ref.shape[1]
    peers, _, halo = outgoing.shape
    ghosts = peers * halo
    own_blocks = cells // LOW
    ghost_blocks = ghosts // LOW
    per = LOW // halo
    chunks = faces // chunk
    d, s = lax.axis_index("dom"), lax.axis_index("sub")
    count = dom * sub
    me = d * sub + s
    barrier = pltpu.get_barrier_semaphore()

    sources = [node_in, index_in, senders_in, receivers_in, edge_in, edge_first_in, edge_second_in,
               edge_bias_in, edge_gain_in, edge_shift_in, node_cot_in, node_first_in, node_second_in,
               node_bias_in, node_gain_in, edge_cot_in]
    targets = [node_ref, index_ref, senders_ref, receivers_ref, edge_ref, edge_first_ref, edge_second_ref,
               edge_bias_ref, edge_gain_ref, edge_shift_ref, node_cot_ref, node_first_ref, node_second_ref,
               node_bias_ref, node_gain_ref, edge_cot_ref]
    loads = [pltpu.make_async_copy(a, b, load_sem.at[i]) for i, (a, b) in enumerate(zip(sources, targets))]
    for load in loads:
        load.start()

    def greet(r, carry):
        other = lax.rem(me + r, count)
        pl.semaphore_signal(
            barrier, inc=1, device_id=(other // sub, lax.rem(other, sub)), device_id_type=MESH
        )
        return carry

    lax.fori_loop(1, count, greet, 0)
    clear_absent(dom, sub, s, incoming, True)
    clear_absent(dom, sub, s, returned, False)
    loads[0].wait()
    loads[1].wait()

    def halves(i):
        return pl.ds(pl.multiple_of(i * LOW, LOW), LOW)

    table = stack_blocks(node_ref[...])

    def pick(i, carry):
        here = halves(i)
        index = index_ref[:, here]
        write_selector(export_sel, here, index)
        export_high[:, here] = high_rows(index)
        picked = choose(nn(table, export_sel[:, here]), high_part(index), 0, jnp.zeros((features, LOW), F32))
        picked = picked.astype(BF)
        for p in range(per):
            outgoing[i * per + p] = picked[:, p * halo : (p + 1) * halo]
        return carry

    for i in range(ghost_blocks):
        pick(i, 0)
    pl.semaphore_wait(barrier, count - 1)
    start_exchange(dom, sub, s, outgoing, incoming, send_sem, recv_sem, forward=True)

    for load in loads[2:]:
        load.wait()
    edge_first_t = edge_first_ref[...]
    edge_first = flip(edge_first_t).astype(BF)
    edge_second = edge_second_ref[...]
    edge_second_t = flip(edge_second).astype(BF)
    vectors = [edge_bias_ref, edge_gain_ref, edge_shift_ref, node_bias_ref, node_gain_ref]
    columns = jnp.concatenate([v[...] for v in vectors] + [jnp.zeros((3, features), F32)], axis=0).T
    edge_bias, edge_gain, edge_shift, node_bias, node_gain = (columns[:, i : i + 1] for i in range(5))

    def span(c):
        return pl.ds(pl.multiple_of(c * chunk, chunk), chunk)

    def prepare(c, carry):
        here = span(c)
        sender = senders_ref[:, here]
        receiver = receivers_ref[:, here]
        write_selector(sender_sel, here, sender)
        write_selector(receiver_sel, here, receiver)
        sender_high[:, here] = high_rows(sender)
        receiver_high[:, here] = high_rows(receiver)
        zero = jnp.zeros((features, chunk), F32)
        received = choose(nn(table, receiver_sel[:, here]), high_part(receiver), 0, zero).astype(BF)
        sent = choose(nn(table, sender_sel[:, here]), high_part(sender), 0, zero).astype(BF)
        stacked[:features, here] = sent
        stacked[features:, here] = received
        slope[:, here] = nn(edge_first_t[:, features:], jnp.concatenate([received, edge_ref[:, here]], axis=0)) + edge_bias
        return carry

    lax.fori_loop(0, chunks, prepare, 0)
    summed[...] = jnp.zeros(summed.shape, F32)
    finish_exchange(dom, sub, s, outgoing, incoming, send_sem, recv_sem, forward=True)
    ghost_table = jnp.concatenate(
        [jnp.concatenate([incoming[i * per + p] for p in range(per)], axis=1) for i in range(ghost_blocks)], axis=0
    )

    def forward(c, carry):
        here = span(c)
        sent = choose(
            nn(ghost_table, sender_sel[:, here]), high_part(senders_ref[:, here]), own_blocks,
            stacked[:features, here].astype(F32),
        ).astype(BF)
        stacked[:features, here] = sent
        lively, steep = lively_and_slope(nn(edge_first_t[:, :features], sent) + slope[:, here])
        lively = lively.astype(BF)
        slope[:, here] = steep
        active[:, here] = lively
        scaled, spread = standardize(nn(edge_second_t, lively))
        scaled_all[:, here] = scaled
        spread_all[:, here] = spread
        message = (scaled * edge_gain + edge_shift).astype(BF)
        message = spread_blocks(message, receiver_high[:, here], range(own_blocks))
        summed[...] += nt(message, receiver_sel[:, here])
        return carry

    lax.fori_loop(0, chunks, forward, 0)

    def unstack(values):
        return jnp.concatenate([values[i : i + features] for i in range(0, values.shape[0], features)], axis=1)

    node_first_t = node_first_ref[...]
    node_first = flip(node_first_t).astype(BF)
    node_second_t = flip(node_second_ref[...]).astype(BF)
    node_input = jnp.concatenate([node_ref[...], unstack(summed[...]).astype(BF)], axis=0)
    node_lively, node_slope = lively_and_slope(nn(node_first_t, node_input) + node_bias)
    node_active = node_lively.astype(BF)
    node_scaled, node_spread = standardize(nn(node_second_t, node_active))
    upstream = node_cot_ref[...].astype(F32)
    node_delta = normalize_back(upstream, node_scaled, node_spread, node_gain).astype(BF)
    node_hidden = nn(node_second_ref[...], node_delta) * node_slope
    lanes[3] = fold_lanes(upstream * node_scaled)
    lanes[4] = fold_lanes(upstream)
    lanes[5] = fold_lanes(node_hidden)
    node_hidden = node_hidden.astype(BF)
    node_back = nn(node_first, node_hidden)
    local[...] = node_back[:features] + upstream
    toward = node_back[features:]
    high = toward.astype(BF)
    low = (toward - high.astype(F32)).astype(BF)
    toward_high, toward_low = stack_blocks(high), stack_blocks(low)

    def columns_of(first):
        column = lax.broadcasted_iota(jnp.int32, (features, 128), 1)
        result = jnp.zeros((features, 128), F32)
        for i in range(3):
            result = jnp.where(column == i, jnp.sum(lanes[first + i], axis=1, keepdims=True), result)
        return result

    def pack(packed, begin, values):
        for j in range(values.shape[0] // PIECE):
            packed[begin + j] = values[j * PIECE : (j + 1) * PIECE].astype(BF)

    edge_number, node_number = edge_packed.shape[0], node_packed.shape[0]
    edge_mine = me - edge_owner(count, 0)
    node_mine = jnp.where(me < 8, me, me - (count - 16))
    edge_reduction = Reduction(
        count, sub, me, edge_number, edge_owner,
        ((edge_mine >= 0) & (edge_mine < edge_number), jnp.clip(edge_mine, 0, edge_number - 1)),
        edge_packed, edge_landing, edge_reduced, edge_sum,
        (edge_part_send, edge_part_recv, edge_whole_send, edge_whole_recv),
    )
    node_reduction = Reduction(
        count, sub, me, node_number, node_owner,
        ((me < 8) | (me >= count - 8), jnp.clip(node_mine, 0, node_number - 1)),
        node_packed, node_landing, node_reduced, node_sum,
        (node_part_send, node_part_recv, node_whole_send, node_whole_recv),
    )
    pack(node_packed, 0, nt(node_hidden, node_input))
    node_right = jnp.concatenate([nt(node_active, node_delta), columns_of(3)[:, :features]], axis=1)
    pack(node_packed, features // PIECE, node_right)
    node_reduction.send_parts()

    grads[...] = jnp.zeros(grads.shape, F32)
    for i in range(3):
        lanes[i] = jnp.zeros(lanes.shape[1:], F32)

    def backward(c, carry):
        here = span(c)
        zero = jnp.zeros((features, chunk), F32)
        gathered = nn(toward_high, receiver_sel[:, here]) + nn(toward_low, receiver_sel[:, here])
        delta = edge_cot_ref[:, here].astype(F32) + choose(gathered, high_part(receivers_ref[:, here]), 0, zero)
        scaled = scaled_all[:, here]
        lanes[0] += fold_lanes(delta * scaled)
        lanes[1] += fold_lanes(delta)
        edge_delta = normalize_back(delta, scaled, spread_all[:, here], edge_gain).astype(BF)
        grads[:, 192:] += nt(active[:, here], edge_delta)
        hidden = nn(edge_second, edge_delta) * slope[:, here]
        lanes[2] += fold_lanes(hidden)
        hidden = hidden.astype(BF)
        active[:, here] = hidden
        grads[:, :128] += nt(hidden, stacked[:, here])
        grads[:, 128:192] += nt(hidden, edge_ref[:, here])
        return carry

    lax.fori_loop(0, chunks, backward, 0)
    pack(edge_packed, 0, grads[:, :128])
    pack(edge_packed, features // PIECE, grads[:, 128:])
    edge_packed[edge_number - 1] = jnp.concatenate(
        [columns_of(0).T[:PIECE], jnp.zeros((PIECE, features), F32)], axis=1
    ).astype(BF)
    edge_reduction.send_parts()

    by_sender[...] = jnp.zeros(by_sender.shape, F32)
    by_receiver[...] = jnp.zeros(by_receiver.shape, F32)
    ghost_rows = ghost_blocks * features

    def scatter_ghosts(c, carry):
        here = span(c)
        values = spread_blocks(active[:, here], sender_high[:, here], range(own_blocks, own_blocks + ghost_blocks))
        by_sender[:ghost_rows] += nt(values, sender_sel[:, here])
        return carry

    lax.fori_loop(0, chunks, scatter_ghosts, 0)
    for i in range(ghost_blocks):
        back = nn(edge_first[:features], by_sender[i * features : (i + 1) * features].astype(BF)).astype(BF)
        for p in range(per):
            returning[i * per + p] = back[:, p * halo : (p + 1) * halo]
    start_exchange(dom, sub, s, returning, returned, back_send, back_recv, forward=False)

    def scatter_own(c, carry):
        here = span(c)
        hidden = active[:, here]
        by_sender[ghost_rows:] += nt(spread_blocks(hidden, sender_high[:, here], range(own_blocks)), sender_sel[:, here])
        by_receiver[...] += nt(spread_blocks(hidden, receiver_high[:, here], range(own_blocks)), receiver_sel[:, here])
        ahead = nn(edge_first[2 * features :], hidden)
        edge_out_ref[:, here] = (edge_cot_ref[:, here].astype(F32) + ahead).astype(BF)
        return carry

    lax.fori_loop(0, chunks, scatter_own, 0)
    both = jnp.concatenate([unstack(by_sender[ghost_rows:]), unstack(by_receiver[...])], axis=0).astype(BF)
    weights = jnp.concatenate([edge_first[:features], edge_first[features : 2 * features]], axis=1)
    local[...] += nn(weights, both)

    node_reduction.reduce()
    finish_exchange(dom, sub, s, returning, returned, back_send, back_recv, forward=False)
    exported = jnp.concatenate([returned[k] for k in range(peers)], axis=1)
    exported = spread_blocks(exported, export_high[...], range(own_blocks))
    state_ref[...] = (local[...] + unstack(nt(exported, export_sel[...]))).astype(BF)
    edge_reduction.reduce()
    settle_exchange(dom, sub, s, outgoing, incoming, send_sem, recv_sem, forward=True)
    settle_exchange(dom, sub, s, returning, returned, back_send, back_recv, forward=False)
    node_reduction.settle()
    edge_reduction.settle()


def unpack_kernel(
    factor, state_in, edge_in, edge_sum, node_sum,
    state_ref, edge_ref, edge_first_ref, edge_second_ref, node_first_ref, node_second_ref,
    edge_gain_ref, edge_shift_ref, edge_bias_ref, node_gain_ref, node_shift_ref, node_bias_ref,
):
    features = state_in.shape[0]
    pieces = features // PIECE
    state_ref[...] = state_in[...]
    edge_ref[...] = edge_in[...]

    def block(ref, begin):
        return jnp.concatenate([ref[begin + j] for j in range(pieces)], axis=0).astype(F32) * factor

    right = block(edge_sum, pieces)
    edge_first_ref[:, : 2 * features] = block(edge_sum, 0)
    edge_first_ref[:, 2 * features :] = right[:, :features]
    edge_second_ref[...] = right[:, features:]
    edge_vectors = edge_sum[2 * pieces].astype(F32) * factor
    node_first_ref[...] = block(node_sum, 0)
    right = block(node_sum, pieces)
    node_second_ref[...] = right[:, :features]
    node_vectors = right.T[features : features + PIECE]
    for i, ref in enumerate((edge_gain_ref, edge_shift_ref, edge_bias_ref)):
        ref[...] = edge_vectors[i : i + 1, :features]
    for i, ref in enumerate((node_gain_ref, node_shift_ref, node_bias_ref)):
        ref[...] = node_vectors[i : i + 1]


def on_device(
    dom, sub,
    node_state, edge_state, senders, receivers, send_index, node_cotangent, edge_cotangent,
    edge_first, edge_bias, edge_second, edge_gain, edge_shift, node_first, node_bias, node_second, node_gain,
):
    features, cells = node_state.shape
    faces = edge_state.shape[1]
    halo = send_index.shape[2]
    peers = 3 * sub
    ghosts = peers * halo
    count = dom * sub
    chunk = math.gcd(faces, 512)
    edge_number = 4 * features // 16 + 1
    node_number = 4 * features // 16
    vmem = pl.BlockSpec(memory_space=pltpu.VMEM)
    hbm = pl.BlockSpec(memory_space=pltpu.HBM)
    shape = jax.ShapeDtypeStruct
    dma = pltpu.SemaphoreType.DMA

    def line(vector):
        return vector.reshape(1, -1)

    operands = (
        node_state, edge_state, line(senders), line(receivers), line(send_index),
        node_cotangent, edge_cotangent, edge_first.T, edge_second, node_first.T, node_second,
        line(edge_bias), line(edge_gain), line(edge_shift), line(node_bias), line(node_gain),
    )
    own_rows = cells // LOW * features
    ghost_rows = ghosts // LOW * features
    state, edge_result, edge_total, node_total = pl.pallas_call(
        functools.partial(layer_kernel, dom, sub, chunk),
        out_shape=(
            shape((features, cells), BF),
            shape((features, faces), BF),
            shape((edge_number, PIECE, 128), BF),
            shape((node_number, PIECE, 128), BF),
        ),
        in_specs=[hbm] * 16,
        out_specs=(vmem,) * 4,
        scratch_shapes=[pltpu.VMEM(x.shape, x.dtype) for x in operands]
        + [pltpu.VMEM((peers, features, halo), BF)] * 4
        + [
            pltpu.VMEM((LOW, ghosts), BF),
            pltpu.VMEM((LOW, faces), BF),
            pltpu.VMEM((LOW, faces), BF),
            pltpu.VMEM((16, faces), BF),
            pltpu.VMEM((16, faces), BF),
            pltpu.VMEM((16, ghosts), BF),
            pltpu.VMEM((2 * features, faces), BF),
            pltpu.VMEM((features, faces), F32),
            pltpu.VMEM((features, faces), BF),
            pltpu.VMEM((features, faces), F32),
            pltpu.VMEM((1, faces), F32),
            pltpu.VMEM((own_rows, LOW), F32),
            pltpu.VMEM((ghost_rows + own_rows, LOW), F32),
            pltpu.VMEM((own_rows, LOW), F32),
            pltpu.VMEM((features, 4 * features), F32),
            pltpu.VMEM((6, features, 128), F32),
            pltpu.VMEM((features, cells), F32),
            pltpu.VMEM((edge_number, PIECE, 128), BF),
            pltpu.VMEM((node_number, PIECE, 128), BF),
            pltpu.VMEM((count, PIECE, 128), BF),
            pltpu.VMEM((count, PIECE, 128), BF),
            pltpu.VMEM((PIECE, 128), BF),
            pltpu.VMEM((PIECE, 128), BF),
        ]
        + [dma((16,))]
        + [dma((peers,))] * 4
        + [dma((edge_number,)), dma((count,)), dma((count,)), dma((edge_number,))]
        + [dma((node_number,)), dma((count,)), dma((count,)), dma((node_number,))],
        compiler_params=pltpu.CompilerParams(
            collective_id=0, has_side_effects=True, vmem_limit_bytes=32 * 1024 * 1024
        ),
        name="layer",
    )(*(pltpu.with_memory_space_constraint(x, pltpu.HBM) for x in operands))
    vector = shape((1, features), F32)
    results = pl.pallas_call(
        functools.partial(unpack_kernel, 1.0 / math.sqrt(faces * count)),
        out_shape=(
            shape((features, cells), BF),
            shape((features, faces), BF),
            shape(edge_first.shape[::-1], F32),
            shape(edge_second.shape, F32),
            shape(node_first.shape[::-1], F32),
            shape(node_second.shape, F32),
        )
        + (vector,) * 6,
        in_specs=[vmem] * 4,
        out_specs=(vmem,) * 12,
        compiler_params=pltpu.CompilerParams(vmem_limit_bytes=16 * 1024 * 1024),
        name="unpack",
    )(state, edge_result, edge_total, node_total)
    state, edge_result, edge_first_sum, edge_second_sum, node_first_sum, node_second_sum, *vectors = results
    vectors = [v.reshape(-1) for v in vectors]
    return (
        state, edge_result, edge_first_sum.T, vectors[2], edge_second_sum, vectors[0], vectors[1],
        node_first_sum.T, vectors[5], node_second_sum, vectors[3], vectors[4],
    )


def solution(mesh):
    split = P(None, ("dom", "sub"))
    faces = P(("dom", "sub"))
    return jax.shard_map(
        functools.partial(on_device, mesh.shape["dom"], mesh.shape["sub"]),
        mesh=mesh,
        in_specs=(split, split, faces, faces, P(("dom", "sub"), None, None), split, split) + (P(),) * 9,
        out_specs=(split, split) + (P(),) * 10,
        check_vma=False,
    )
```

time: 51.7 us -> 36.9 us (0.71)
  Pallas kernels: 50.9 us -> 36.1 us
    pallas_call x1, Pallas kernels: 48.8 us -> 35.2 us  [on_device(): pl.pallas_call(functools.partial(layer_kernel, dom, sub, chunk), out_shap...]
    pallas_call x1, Pallas kernels: 2.09 us -> 0.88 us  [on_device(): pl.pallas_call(functools.partial(unpack_kernel, 1.0 / math.sqrt(faces * c...]
where the time goes in v1:
time: 36.9 us; the launch traced here: 36.8 us
  Pallas kernels  36.1 us (98%)
  between operations  0.66 us (2%)
    pallas_call x1, Pallas kernels, on_device(): pl.pallas_call(functools.partial(layer_kernel, dom, sub, chunk), out_shap...  35.2 us
    pallas_call x1, Pallas kernels, on_device(): pl.pallas_call(functools.partial(unpack_kernel, 1.0 / math.sqrt(faces * c...  0.88 us

profile of v1, /device:TPU:0, one launch (start us, length us, event | category | flops | bytes accessed | tf_op | source)
XLA Modules:
  0.0 36.8 jit_solution(13136100774603731346)
XLA Ops:
  0.7 35.2 %layer.1 = (bf16[64,1024]{1,0:T(8,128)(2,1)S(1)}, bf16[64,3072]{1,0:T(8,128)(2,1)S(1)}, bf16[17,8,128]{2,1,0:T(8,128)(2,1)S(1)}, bf16[16,8,128]{2,1,0:T(8,128)(2,1)S(1)}) custom-call(bf16[64,1024]{1,0:T(8,128)(2,1)} %node_in.1, bf16[64,3072]{1,0:T(8,128)(2,1)} %edge_in.1, s32[1,3072]{1,0:T(1,128)} %bitcast.20, s32[1,3072]{1,0:T(1,128)} %bitcast.21, ...), custom_call_target="tpu_custom_call" | custom-call | tf_op jit(solution)/shard_map/layer/pallas_call | solution.py:574
  35.9 0.9 %unpack.1 = (bf16[64,1024]{1,0:T(8,128)(2,1)}, bf16[64,3072]{1,0:T(8,128)(2,1)}, f32[64,192]{1,0:T(8,128)}, f32[64,64]{1,0:T(8,128)}, f32[64,128]{1,0:T(8,128)},...) custom-call(bf16[64,1024]{1,0:T(8,128)(2,1)S(1)} %get-tuple-element., ...), custom_call_target="tpu_custom_call" | custom-call | tf_op jit(solution)/shard_map/unpack/pallas_call | solution.py:621

commit v2 on v1

--- a/solution.py
+++ b/solution.py
@@ -105,17 +105,6 @@
             yield o, t, target, (target >= 0) & (target < dom)
 
 
-def halo_copy(outgoing, incoming, send_sem, recv_sem, source, landing, target, t):
-    return pltpu.make_async_remote_copy(
-        src_ref=outgoing.at[source],
-        dst_ref=incoming.at[landing],
-        send_sem=send_sem.at[source],
-        recv_sem=recv_sem.at[landing],
-        device_id=(target, t),
-        device_id_type=MESH,
-    )
-
-
 def guarded(o, there, action):
     if o == 1:
         action()
@@ -128,7 +117,14 @@
         block = o if forward else 2 - o
 
         def start(block=block, t=t, target=target):
-            halo_copy(outgoing, incoming, send_sem, recv_sem, block * sub + t, block * sub + s, target, t).start()
+            pltpu.make_async_remote_copy(
+                src_ref=outgoing.at[block * sub + t],
+                dst_ref=incoming.at[block * sub + s],
+                send_sem=send_sem.at[block],
+                recv_sem=recv_sem.at[block],
+                device_id=(target, t),
+                device_id_type=MESH,
+            ).start()
 
         guarded(o, there, start)
 
@@ -145,24 +141,20 @@
                 incoming[o * sub + u] = jnp.zeros(incoming.shape[1:], incoming.dtype)
 
 
-def finish_exchange(dom, sub, s, outgoing, incoming, send_sem, recv_sem, forward):
-    for o, t, target, there in halo_peers(dom, sub):
-        block = 2 - o if forward else o
-
-        def finish(block=block, t=t, target=target):
-            halo_copy(outgoing, incoming, send_sem, recv_sem, block * sub + t, block * sub + t, target, t).wait_recv()
-
-        guarded(o, there, finish)
-
-
-def settle_exchange(dom, sub, s, outgoing, incoming, send_sem, recv_sem, forward):
-    for o, t, target, there in halo_peers(dom, sub):
-        block = o if forward else 2 - o
-
-        def finish(block=block, t=t, target=target):
-            halo_copy(outgoing, incoming, send_sem, recv_sem, block * sub + t, block * sub + t, target, t).wait_send()
-
-        guarded(o, there, finish)
+def await_bytes(ref, sem):
+    pltpu.make_async_copy(ref, ref, sem).wait()
+
+
+def settle_exchange(dom, sub, blocks, sem, ahead):
+    d = lax.axis_index("dom")
+    for o in (1, 0, 2):
+        row = d + o - 1 if ahead else d + 1 - o
+        number = sub - 1 if o == 1 else sub
+
+        def finish(o=o, number=number):
+            await_bytes(blocks.at[pl.ds(o * sub, number)], sem.at[o])
+
+        guarded(o, (row >= 0) & (row < dom), finish)
 
 
 def edge_owner(count, j):
@@ -170,39 +162,18 @@
 
 
 def node_owner(count, j):
-    return j + jnp.where(j < 8, 0, count - 16) if not isinstance(j, int) else (j if j < 8 else count - 16 + j)
+    return jnp.where(j < 8, j, count - 16 + j)
 
 
 class Reduction:
-    def __init__(self, count, sub, me, number, owner, owned, packed, landing, reduced, result, sems):
+    def __init__(self, count, sub, me, owner, is_owner, mine, packed, landing, reduced, result, sems):
         self.count, self.sub, self.me = count, sub, me
-        self.number, self.owner, self.owned = number, owner, owned
-        self.packed, self.landing, self.reduced, self.result = packed, landing, reduced, result
-        self.part_send, self.part_recv, self.whole_send, self.whole_recv = sems
-        self.is_owner, self.mine = owned
+        self.number = packed.shape[0]
+        self.owner, self.is_owner, self.mine = owner, is_owner, jnp.clip(mine, 0, self.number - 1)
+        self.packed, self.landing, self.reduced, self.result, self.sems = packed, landing, reduced, result, sems
 
     def device(self, rank):
         return (rank // self.sub, lax.rem(rank, self.sub))
-
-    def part(self, j, source, rank):
-        return pltpu.make_async_remote_copy(
-            src_ref=self.packed.at[j],
-            dst_ref=self.landing.at[source],
-            send_sem=self.part_send.at[j],
-            recv_sem=self.part_recv.at[source],
-            device_id=self.device(rank),
-            device_id_type=MESH,
-        )
-
-    def whole(self, j, rank):
-        return pltpu.make_async_remote_copy(
-            src_ref=self.reduced,
-            dst_ref=self.result.at[j],
-            send_sem=self.whole_send.at[rank],
-            recv_sem=self.whole_recv.at[j],
-            device_id=self.device(rank),
-            device_id_type=MESH,
-        )
 
     def send_parts(self):
         def body(j, carry):
@@ -210,49 +181,52 @@
 
             @pl.when(rank != self.me)
             def _():
-                self.part(j, self.me, rank).start()
+                pltpu.make_async_remote_copy(
+                    src_ref=self.packed.at[j],
+                    dst_ref=self.landing.at[lax.rem(self.me - rank + self.count, self.count) - 1],
+                    send_sem=self.sems.at[0],
+                    recv_sem=self.sems.at[1],
+                    device_id=self.device(rank),
+                    device_id_type=MESH,
+                ).start()
 
             return carry
 
         lax.fori_loop(0, self.number, body, 0)
-
-    def others(self, action):
-        def body(r, carry):
-            rank = lax.rem(self.me + r, self.count)
-            action(rank)
-            return carry
-
-        lax.fori_loop(1, self.count, body, 0)
 
     def reduce(self):
         @pl.when(self.is_owner)
         def _():
-            def take(r, total):
-                rank = lax.rem(self.me + r, self.count)
-                self.part(self.mine, rank, rank).wait_recv()
-                return total + self.landing[rank].astype(F32)
-
-            total = lax.fori_loop(1, self.count, take, self.packed[self.mine].astype(F32))
+            await_bytes(self.landing, self.sems.at[1])
+            total = self.packed[self.mine].astype(F32) + jnp.sum(self.landing[...].astype(F32), axis=0)
             self.reduced[...] = total.astype(BF)
             self.result[self.mine] = total.astype(BF)
-            self.others(lambda rank: self.whole(self.mine, rank).start())
+
+            def body(k, carry):
+                rank = lax.rem(self.me + 1 + lax.rem(k + self.count // 2, self.count - 1), self.count)
+                pltpu.make_async_remote_copy(
+                    src_ref=self.reduced,
+                    dst_ref=self.result.at[self.mine],
+                    send_sem=self.sems.at[2],
+                    recv_sem=self.sems.at[3],
+                    device_id=self.device(rank),
+                    device_id_type=MESH,
+                ).start()
+                return carry
+
+            lax.fori_loop(0, self.count - 1, body, 0)
 
     def settle(self):
-        def body(j, carry):
-            rank = self.owner(self.count, j)
-
-            @pl.when(rank != self.me)
-            def _():
-                self.part(j, rank, rank).wait_send()
-                self.whole(j, rank).wait_recv()
-
-            return carry
-
-        lax.fori_loop(0, self.number, body, 0)
-
         @pl.when(self.is_owner)
         def _():
-            self.others(lambda rank: self.whole(self.mine, rank).wait_send())
+            await_bytes(self.packed.at[pl.ds(0, self.number - 1)], self.sems.at[0])
+            await_bytes(self.landing, self.sems.at[2])
+            await_bytes(self.result.at[pl.ds(0, self.number - 1)], self.sems.at[3])
+
+        @pl.when(jnp.logical_not(self.is_owner))
+        def _():
+            await_bytes(self.packed, self.sems.at[0])
+            await_bytes(self.result, self.sems.at[3])
 
 
 def layer_kernel(
@@ -269,8 +243,7 @@
     stacked, slope, active, scaled_all, spread_all, summed, by_sender, by_receiver, grads, lanes, local,
     edge_packed, node_packed, edge_landing, node_landing, edge_reduced, node_reduced,
     load_sem, send_sem, recv_sem, back_send, back_recv,
-    edge_part_send, edge_part_recv, edge_whole_send, edge_whole_recv,
-    node_part_send, node_part_recv, node_whole_send, node_whole_recv,
+    edge_sems, node_sems,
 ):
     features, cells = node_ref.shape
     faces = edge_ref.shape[1]
@@ -342,31 +315,29 @@
     def span(c):
         return pl.ds(pl.multiple_of(c * chunk, chunk), chunk)
 
-    def prepare(c, carry):
-        here = span(c)
+    everything = pl.ds(0, faces)
+
+    def prepare(here):
         sender = senders_ref[:, here]
         receiver = receivers_ref[:, here]
         write_selector(sender_sel, here, sender)
         write_selector(receiver_sel, here, receiver)
         sender_high[:, here] = high_rows(sender)
         receiver_high[:, here] = high_rows(receiver)
-        zero = jnp.zeros((features, chunk), F32)
+        zero = jnp.zeros((features, faces), F32)
         received = choose(nn(table, receiver_sel[:, here]), high_part(receiver), 0, zero).astype(BF)
         sent = choose(nn(table, sender_sel[:, here]), high_part(sender), 0, zero).astype(BF)
         stacked[:features, here] = sent
         stacked[features:, here] = received
         slope[:, here] = nn(edge_first_t[:, features:], jnp.concatenate([received, edge_ref[:, here]], axis=0)) + edge_bias
-        return carry
-
-    lax.fori_loop(0, chunks, prepare, 0)
-    summed[...] = jnp.zeros(summed.shape, F32)
-    finish_exchange(dom, sub, s, outgoing, incoming, send_sem, recv_sem, forward=True)
+
+    prepare(everything)
+    settle_exchange(dom, sub, incoming, recv_sem, False)
     ghost_table = jnp.concatenate(
         [jnp.concatenate([incoming[i * per + p] for p in range(per)], axis=1) for i in range(ghost_blocks)], axis=0
     )
 
-    def forward(c, carry):
-        here = span(c)
+    def forward(here):
         sent = choose(
             nn(ghost_table, sender_sel[:, here]), high_part(senders_ref[:, here]), own_blocks,
             stacked[:features, here].astype(F32),
@@ -381,10 +352,9 @@
         spread_all[:, here] = spread
         message = (scaled * edge_gain + edge_shift).astype(BF)
         message = spread_blocks(message, receiver_high[:, here], range(own_blocks))
-        summed[...] += nt(message, receiver_sel[:, here])
-        return carry
-
-    lax.fori_loop(0, chunks, forward, 0)
+        summed[...] = nt(message, receiver_sel[:, here])
+
+    forward(everything)
 
     def unstack(values):
         return jnp.concatenate([values[i : i + features] for i in range(0, values.shape[0], features)], axis=1)
@@ -421,49 +391,39 @@
         for j in range(values.shape[0] // PIECE):
             packed[begin + j] = values[j * PIECE : (j + 1) * PIECE].astype(BF)
 
-    edge_number, node_number = edge_packed.shape[0], node_packed.shape[0]
+    edge_number = edge_packed.shape[0]
     edge_mine = me - edge_owner(count, 0)
-    node_mine = jnp.where(me < 8, me, me - (count - 16))
     edge_reduction = Reduction(
-        count, sub, me, edge_number, edge_owner,
-        ((edge_mine >= 0) & (edge_mine < edge_number), jnp.clip(edge_mine, 0, edge_number - 1)),
-        edge_packed, edge_landing, edge_reduced, edge_sum,
-        (edge_part_send, edge_part_recv, edge_whole_send, edge_whole_recv),
+        count, sub, me, edge_owner, (edge_mine >= 0) & (edge_mine < edge_number), edge_mine,
+        edge_packed, edge_landing, edge_reduced, edge_sum, edge_sems,
     )
     node_reduction = Reduction(
-        count, sub, me, node_number, node_owner,
-        ((me < 8) | (me >= count - 8), jnp.clip(node_mine, 0, node_number - 1)),
-        node_packed, node_landing, node_reduced, node_sum,
-        (node_part_send, node_part_recv, node_whole_send, node_whole_recv),
+        count, sub, me, node_owner, (me < 8) | (me >= count - 8), jnp.where(me < 8, me, me - (count - 16)),
+        node_packed, node_landing, node_reduced, node_sum, node_sems,
     )
     pack(node_packed, 0, nt(node_hidden, node_input))
     node_right = jnp.concatenate([nt(node_active, node_delta), columns_of(3)[:, :features]], axis=1)
     pack(node_packed, features // PIECE, node_right)
     node_reduction.send_parts()
 
-    grads[...] = jnp.zeros(grads.shape, F32)
-    for i in range(3):
-        lanes[i] = jnp.zeros(lanes.shape[1:], F32)
-
-    def backward(c, carry):
-        here = span(c)
-        zero = jnp.zeros((features, chunk), F32)
+
+    def backward(here):
+        zero = jnp.zeros((features, faces), F32)
         gathered = nn(toward_high, receiver_sel[:, here]) + nn(toward_low, receiver_sel[:, here])
         delta = edge_cot_ref[:, here].astype(F32) + choose(gathered, high_part(receivers_ref[:, here]), 0, zero)
         scaled = scaled_all[:, here]
-        lanes[0] += fold_lanes(delta * scaled)
-        lanes[1] += fold_lanes(delta)
+        lanes[0] = fold_lanes(delta * scaled)
+        lanes[1] = fold_lanes(delta)
         edge_delta = normalize_back(delta, scaled, spread_all[:, here], edge_gain).astype(BF)
-        grads[:, 192:] += nt(active[:, here], edge_delta)
+        grads[:, 192:] = nt(active[:, here], edge_delta)
         hidden = nn(edge_second, edge_delta) * slope[:, here]
-        lanes[2] += fold_lanes(hidden)
+        lanes[2] = fold_lanes(hidden)
         hidden = hidden.astype(BF)
         active[:, here] = hidden
-        grads[:, :128] += nt(hidden, stacked[:, here])
-        grads[:, 128:192] += nt(hidden, edge_ref[:, here])
-        return carry
-
-    lax.fori_loop(0, chunks, backward, 0)
+        grads[:, :128] = nt(hidden, stacked[:, here])
+        grads[:, 128:192] = nt(hidden, edge_ref[:, here])
+
+    backward(everything)
     pack(edge_packed, 0, grads[:, :128])
     pack(edge_packed, features // PIECE, grads[:, 128:])
     edge_packed[edge_number - 1] = jnp.concatenate(
@@ -503,13 +463,13 @@
     local[...] += nn(weights, both)
 
     node_reduction.reduce()
-    finish_exchange(dom, sub, s, returning, returned, back_send, back_recv, forward=False)
+    edge_reduction.reduce()
+    settle_exchange(dom, sub, returned, back_recv, True)
     exported = jnp.concatenate([returned[k] for k in range(peers)], axis=1)
     exported = spread_blocks(exported, export_high[...], range(own_blocks))
     state_ref[...] = (local[...] + unstack(nt(exported, export_sel[...]))).astype(BF)
-    edge_reduction.reduce()
-    settle_exchange(dom, sub, s, outgoing, incoming, send_sem, recv_sem, forward=True)
-    settle_exchange(dom, sub, s, returning, returned, back_send, back_recv, forward=False)
+    settle_exchange(dom, sub, outgoing, send_sem, True)
+    settle_exchange(dom, sub, returning, back_send, False)
     node_reduction.settle()
     edge_reduction.settle()
 
@@ -553,7 +513,7 @@
     peers = 3 * sub
     ghosts = peers * halo
     count = dom * sub
-    chunk = math.gcd(faces, 512)
+    chunk = math.gcd(faces, 1536)
     edge_number = 4 * features // 16 + 1
     node_number = 4 * features // 16
     vmem = pl.BlockSpec(memory_space=pltpu.VMEM)
@@ -603,15 +563,14 @@
             pltpu.VMEM((features, cells), F32),
             pltpu.VMEM((edge_number, PIECE, 128), BF),
             pltpu.VMEM((node_number, PIECE, 128), BF),
-            pltpu.VMEM((count, PIECE, 128), BF),
-            pltpu.VMEM((count, PIECE, 128), BF),
+            pltpu.VMEM((count - 1, PIECE, 128), BF),
+            pltpu.VMEM((count - 1, PIECE, 128), BF),
             pltpu.VMEM((PIECE, 128), BF),
             pltpu.VMEM((PIECE, 128), BF),
         ]
         + [dma((16,))]
-        + [dma((peers,))] * 4
-        + [dma((edge_number,)), dma((count,)), dma((count,)), dma((edge_number,))]
-        + [dma((node_number,)), dma((count,)), dma((count,)), dma((node_number,))],
+        + [dma((3,))] * 4
+        + [dma((4,))] * 2,
         compiler_params=pltpu.CompilerParams(
             collective_id=0, has_side_effects=True, vmem_limit_bytes=32 * 1024 * 1024
         ),

time: 36.9 us -> 27.8 us (0.75)
  Pallas kernels: 36.1 us -> 27 us
    pallas_call x1, Pallas kernels: 35.2 us -> 26.1 us  [on_device(): pl.pallas_call(functools.partial(layer_kernel, dom, sub, chunk), out_shap...]
where the time goes in v2:
time: 27.8 us; the launch traced here: 27.6 us
  Pallas kernels  27 us (97%)
  between operations  0.66 us (2%)
    pallas_call x1, Pallas kernels, on_device(): pl.pallas_call(functools.partial(layer_kernel, dom, sub, chunk), out_shap...  26.1 us
    pallas_call x1, Pallas kernels, on_device(): pl.pallas_call(functools.partial(unpack_kernel, 1.0 / math.sqrt(faces * c...  0.88 us

profile of v2, /device:TPU:0, one launch (start us, length us, event | category | flops | bytes accessed | tf_op | source)
XLA Modules:
  0.0 27.6 jit_solution(8913822999354021133)
XLA Ops:
  0.7 26.1 %layer.1 = (bf16[64,1024]{1,0:T(8,128)(2,1)S(1)}, bf16[64,3072]{1,0:T(8,128)(2,1)S(1)}, bf16[17,8,128]{2,1,0:T(8,128)(2,1)S(1)}, bf16[16,8,128]{2,1,0:T(8,128)(2,1)S(1)}) custom-call(bf16[64,1024]{1,0:T(8,128)(2,1)} %node_in.1, bf16[64,3072]{1,0:T(8,128)(2,1)} %edge_in.1, s32[1,3072]{1,0:T(1,128)} %bitcast.20, s32[1,3072]{1,0:T(1,128)} %bitcast.21, ...), custom_call_target="tpu_custom_call" | custom-call | tf_op jit(solution)/shard_map/layer/pallas_call | solution.py:534
  26.7 0.9 %unpack.1 = (bf16[64,1024]{1,0:T(8,128)(2,1)}, bf16[64,3072]{1,0:T(8,128)(2,1)}, f32[64,192]{1,0:T(8,128)}, f32[64,64]{1,0:T(8,128)}, f32[64,128]{1,0:T(8,128)},...) custom-call(bf16[64,1024]{1,0:T(8,128)(2,1)S(1)} %get-tuple-element., ...), custom_call_target="tpu_custom_call" | custom-call | tf_op jit(solution)/shard_map/unpack/pallas_call | solution.py:580

commit v3 on v2

--- a/solution.py
+++ b/solution.py
@@ -13,7 +13,7 @@
 BF = jnp.bfloat16
 F32 = jnp.float32
 LOW = 256
-PIECE = 8
+PIECE = 16
 
 
 def nn(a, b):
@@ -112,8 +112,10 @@
         pl.when(there)(action)
 
 
-def start_exchange(dom, sub, s, outgoing, incoming, send_sem, recv_sem, forward):
+def start_exchange(dom, sub, s, outgoing, incoming, send_sem, recv_sem, forward, only=(0, 2, 1)):
     for o, t, target, there in halo_peers(dom, sub):
+        if o not in only:
+            continue
         block = o if forward else 2 - o
 
         def start(block=block, t=t, target=target):
@@ -129,6 +131,36 @@
         guarded(o, there, start)
 
 
+def reaches(dom):
+    reach = 1
+    while reach < dom - 1:
+        yield reach
+        reach *= 2
+
+
+def announce(dom, sem, level, reach):
+    d, s = lax.axis_index("dom"), lax.axis_index("sub")
+    for row in (d - reach, d + reach):
+
+        @pl.when((row >= 0) & (row < dom))
+        def _():
+            pl.semaphore_signal(sem.at[level], inc=1, device_id=(row, s), device_id_type=MESH)
+
+
+def hear(dom, sem, level, reach):
+    d = lax.axis_index("dom")
+    number = jnp.where(d >= reach, 1, 0) + jnp.where(d + reach < dom, 1, 0)
+    pl.semaphore_wait(sem.at[level], number)
+
+
+def repeat(number, body):
+    if number <= 32:
+        for k in range(number):
+            body(k)
+    else:
+        lax.fori_loop(0, number, lambda k, carry: (body(k), carry)[1], 0)
+
+
 def clear_absent(dom, sub, s, incoming, forward):
     d = lax.axis_index("dom")
     incoming[sub + s] = jnp.zeros(incoming.shape[1:], incoming.dtype)
@@ -145,9 +177,9 @@
     pltpu.make_async_copy(ref, ref, sem).wait()
 
 
-def settle_exchange(dom, sub, blocks, sem, ahead):
+def settle_exchange(dom, sub, blocks, sem, ahead, only=(1, 0, 2)):
     d = lax.axis_index("dom")
-    for o in (1, 0, 2):
+    for o in only:
         row = d + o - 1 if ahead else d + 1 - o
         number = sub - 1 if o == 1 else sub
 
@@ -158,11 +190,11 @@
 
 
 def edge_owner(count, j):
-    return count // 2 - 8 + j
+    return count // 2 - 4 + j
 
 
 def node_owner(count, j):
-    return jnp.where(j < 8, j, count - 16 + j)
+    return count // 2 + (j - 8 if j < 4 else j)
 
 
 class Reduction:
@@ -176,7 +208,7 @@
         return (rank // self.sub, lax.rem(rank, self.sub))
 
     def send_parts(self):
-        def body(j, carry):
+        for j in range(self.number):
             rank = self.owner(self.count, j)
 
             @pl.when(rank != self.me)
@@ -190,10 +222,6 @@
                     device_id_type=MESH,
                 ).start()
 
-            return carry
-
-        lax.fori_loop(0, self.number, body, 0)
-
     def reduce(self):
         @pl.when(self.is_owner)
         def _():
@@ -202,7 +230,7 @@
             self.reduced[...] = total.astype(BF)
             self.result[self.mine] = total.astype(BF)
 
-            def body(k, carry):
+            def body(k):
                 rank = lax.rem(self.me + 1 + lax.rem(k + self.count // 2, self.count - 1), self.count)
                 pltpu.make_async_remote_copy(
                     src_ref=self.reduced,
@@ -212,9 +240,8 @@
                     device_id=self.device(rank),
                     device_id_type=MESH,
                 ).start()
-                return carry
-
-            lax.fori_loop(0, self.count - 1, body, 0)
+
+            repeat(self.count - 1, body)
 
     def settle(self):
         @pl.when(self.is_owner)
@@ -243,7 +270,7 @@
     stacked, slope, active, scaled_all, spread_all, summed, by_sender, by_receiver, grads, lanes, local,
     edge_packed, node_packed, edge_landing, node_landing, edge_reduced, node_reduced,
     load_sem, send_sem, recv_sem, back_send, back_recv,
-    edge_sems, node_sems,
+    edge_sems, node_sems, known,
 ):
     features, cells = node_ref.shape
     faces = edge_ref.shape[1]
@@ -268,14 +295,13 @@
     for load in loads:
         load.start()
 
-    def greet(r, carry):
-        other = lax.rem(me + r, count)
-        pl.semaphore_signal(
-            barrier, inc=1, device_id=(other // sub, lax.rem(other, sub)), device_id_type=MESH
-        )
-        return carry
-
-    lax.fori_loop(1, count, greet, 0)
+    for o, t, target, there in halo_peers(dom, sub):
+
+        def greet(t=t, target=target):
+            pl.semaphore_signal(barrier, inc=1, device_id=(target, t), device_id_type=MESH)
+
+        guarded(o, there, greet)
+    neighbours = sub - 1 + jnp.where(d > 0, sub, 0) + jnp.where(d < dom - 1, sub, 0)
     clear_absent(dom, sub, s, incoming, True)
     clear_absent(dom, sub, s, returned, False)
     loads[0].wait()
@@ -286,8 +312,8 @@
 
     table = stack_blocks(node_ref[...])
 
-    def pick(i, carry):
-        here = halves(i)
+    def pick(i):
+        here = pl.ds(i * LOW, LOW)
         index = index_ref[:, here]
         write_selector(export_sel, here, index)
         export_high[:, here] = high_rows(index)
@@ -295,12 +321,17 @@
         picked = picked.astype(BF)
         for p in range(per):
             outgoing[i * per + p] = picked[:, p * halo : (p + 1) * halo]
-        return carry
-
-    for i in range(ghost_blocks):
-        pick(i, 0)
-    pl.semaphore_wait(barrier, count - 1)
-    start_exchange(dom, sub, s, outgoing, incoming, send_sem, recv_sem, forward=True)
+
+    third = ghost_blocks // 3
+    for o in (0, 2, 1):
+        for i in range(o * third, (o + 1) * third):
+            pick(i)
+        if o == 0:
+            pl.semaphore_wait(barrier, neighbours)
+        start_exchange(dom, sub, s, outgoing, incoming, send_sem, recv_sem, True, (o,))
+    levels = list(enumerate(reaches(dom)))
+    for level, reach in levels[:1]:
+        announce(dom, known, level, reach)
 
     for load in loads[2:]:
         load.wait()
@@ -332,16 +363,33 @@
         slope[:, here] = nn(edge_first_t[:, features:], jnp.concatenate([received, edge_ref[:, here]], axis=0)) + edge_bias
 
     prepare(everything)
-    settle_exchange(dom, sub, incoming, recv_sem, False)
-    ghost_table = jnp.concatenate(
-        [jnp.concatenate([incoming[i * per + p] for p in range(per)], axis=1) for i in range(ghost_blocks)], axis=0
-    )
+    for (level, reach), (after, further) in zip(levels[:1], levels[1:2]):
+        hear(dom, known, level, reach)
+        announce(dom, known, after, further)
+
+    def ghosts_of(o):
+        def block(i):
+            return jnp.concatenate([incoming[i * per + p] for p in range(per)], axis=1)
+
+        return jnp.concatenate([block(i) for i in range(o * third, (o + 1) * third)], axis=0)
+
+    def gather_ghosts(o):
+        settle_exchange(dom, sub, incoming, recv_sem, False, (o,))
+        high = high_part(senders_ref[...])
+        base = stacked[:features].astype(F32)
+        return choose(nn(ghosts_of(o), sender_sel[...]), high, own_blocks + o * third, base).astype(BF)
+
+    for o in (1, 0):
+        stacked[:features] = gather_ghosts(o)
+    settle_exchange(dom, sub, incoming, recv_sem, False, (2,))
+    for (level, reach), (after, further) in zip(levels[1:], levels[2:]):
+        hear(dom, known, level, reach)
+        announce(dom, known, after, further)
 
     def forward(here):
-        sent = choose(
-            nn(ghost_table, sender_sel[:, here]), high_part(senders_ref[:, here]), own_blocks,
-            stacked[:features, here].astype(F32),
-        ).astype(BF)
+        high = high_part(senders_ref[:, here])
+        base = stacked[:features, here].astype(F32)
+        sent = choose(nn(ghosts_of(2), sender_sel[:, here]), high, own_blocks + 2 * third, base).astype(BF)
         stacked[:features, here] = sent
         lively, steep = lively_and_slope(nn(edge_first_t[:, :features], sent) + slope[:, here])
         lively = lively.astype(BF)
@@ -375,10 +423,7 @@
     node_hidden = node_hidden.astype(BF)
     node_back = nn(node_first, node_hidden)
     local[...] = node_back[:features] + upstream
-    toward = node_back[features:]
-    high = toward.astype(BF)
-    low = (toward - high.astype(F32)).astype(BF)
-    toward_high, toward_low = stack_blocks(high), stack_blocks(low)
+    toward = stack_blocks(node_back[features:].astype(BF))
 
     def columns_of(first):
         column = lax.broadcasted_iota(jnp.int32, (features, 128), 1)
@@ -392,24 +437,27 @@
             packed[begin + j] = values[j * PIECE : (j + 1) * PIECE].astype(BF)
 
     edge_number = edge_packed.shape[0]
+    half = count // 2
     edge_mine = me - edge_owner(count, 0)
     edge_reduction = Reduction(
         count, sub, me, edge_owner, (edge_mine >= 0) & (edge_mine < edge_number), edge_mine,
         edge_packed, edge_landing, edge_reduced, edge_sum, edge_sems,
     )
     node_reduction = Reduction(
-        count, sub, me, node_owner, (me < 8) | (me >= count - 8), jnp.where(me < 8, me, me - (count - 16)),
-        node_packed, node_landing, node_reduced, node_sum, node_sems,
+        count, sub, me, node_owner, ((me >= half - 8) & (me < half - 4)) | ((me >= half + 4) & (me < half + 8)),
+        jnp.where(me < half, me - half + 8, me - half), node_packed, node_landing, node_reduced, node_sum, node_sems,
     )
     pack(node_packed, 0, nt(node_hidden, node_input))
     node_right = jnp.concatenate([nt(node_active, node_delta), columns_of(3)[:, :features]], axis=1)
     pack(node_packed, features // PIECE, node_right)
+    for level, reach in levels[-1:]:
+        hear(dom, known, level, reach)
     node_reduction.send_parts()
 
 
     def backward(here):
         zero = jnp.zeros((features, faces), F32)
-        gathered = nn(toward_high, receiver_sel[:, here]) + nn(toward_low, receiver_sel[:, here])
+        gathered = nn(toward, receiver_sel[:, here])
         delta = edge_cot_ref[:, here].astype(F32) + choose(gathered, high_part(receivers_ref[:, here]), 0, zero)
         scaled = scaled_all[:, here]
         lanes[0] = fold_lanes(delta * scaled)
@@ -427,7 +475,7 @@
     pack(edge_packed, 0, grads[:, :128])
     pack(edge_packed, features // PIECE, grads[:, 128:])
     edge_packed[edge_number - 1] = jnp.concatenate(
-        [columns_of(0).T[:PIECE], jnp.zeros((PIECE, features), F32)], axis=1
+        [columns_of(0).T[:PIECE], jnp.zeros((PIECE, 128 - features), F32)], axis=1
     ).astype(BF)
     edge_reduction.send_parts()
 
@@ -495,7 +543,7 @@
     node_first_ref[...] = block(node_sum, 0)
     right = block(node_sum, pieces)
     node_second_ref[...] = right[:, :features]
-    node_vectors = right.T[features : features + PIECE]
+    node_vectors = right.T[features : features + 8]
     for i, ref in enumerate((edge_gain_ref, edge_shift_ref, edge_bias_ref)):
         ref[...] = edge_vectors[i : i + 1, :features]
     for i, ref in enumerate((node_gain_ref, node_shift_ref, node_bias_ref)):
@@ -514,8 +562,8 @@
     ghosts = peers * halo
     count = dom * sub
     chunk = math.gcd(faces, 1536)
-    edge_number = 4 * features // 16 + 1
-    node_number = 4 * features // 16
+    edge_number = 2 * features // PIECE + 1
+    node_number = 2 * features // PIECE
     vmem = pl.BlockSpec(memory_space=pltpu.VMEM)
     hbm = pl.BlockSpec(memory_space=pltpu.HBM)
     shape = jax.ShapeDtypeStruct
@@ -570,7 +618,8 @@
         ]
         + [dma((16,))]
         + [dma((3,))] * 4
-        + [dma((4,))] * 2,
+        + [dma((4,))] * 2
+        + [pltpu.SemaphoreType.REGULAR((max(1, len(list(reaches(dom)))),))],
         compiler_params=pltpu.CompilerParams(
             collective_id=0, has_side_effects=True, vmem_limit_bytes=32 * 1024 * 1024
         ),

time: 27.8 us -> 26.6 us (0.957)
  Pallas kernels: 27 us -> 25.8 us
    pallas_call x1, Pallas kernels: 26.1 us -> 24.9 us  [on_device(): pl.pallas_call(functools.partial(layer_kernel, dom, sub, chunk), out_shap...]
where the time goes in v3:
time: 26.6 us; the launch traced here: 26.5 us
  Pallas kernels  25.8 us (97%)
  between operations  0.66 us (2%)
    pallas_call x1, Pallas kernels, on_device(): pl.pallas_call(functools.partial(layer_kernel, dom, sub, chunk), out_shap...  24.9 us
    pallas_call x1, Pallas kernels, on_device(): pl.pallas_call(functools.partial(unpack_kernel, 1.0 / math.sqrt(faces * c...  0.88 us

profile of v3, /device:TPU:0, one launch (start us, length us, event | category | flops | bytes accessed | tf_op | source)
XLA Modules:
  0.0 26.5 jit_solution(14220318728611256840)
XLA Ops:
  0.7 24.9 %layer.1 = (bf16[64,1024]{1,0:T(8,128)(2,1)S(1)}, bf16[64,3072]{1,0:T(8,128)(2,1)S(1)}, bf16[9,16,128]{2,1,0:T(8,128)(2,1)S(1)}, bf16[8,16,128]{2,1,0:T(8,128)(2,1)S(1)}) custom-call(bf16[64,1024]{1,0:T(8,128)(2,1)} %node_in.1, bf16[64,3072]{1,0:T(8,128)(2,1)} %edge_in.1, s32[1,3072]{1,0:T(1,128)} %bitcast.20, s32[1,3072]{1,0:T(1,128)} %bitcast.21, ...), custom_call_target="tpu_custom_call" | custom-call | tf_op jit(solution)/shard_map/layer/pallas_call | solution.py:582
  25.6 0.9 %unpack.1 = (bf16[64,1024]{1,0:T(8,128)(2,1)}, bf16[64,3072]{1,0:T(8,128)(2,1)}, f32[64,192]{1,0:T(8,128)}, f32[64,64]{1,0:T(8,128)}, f32[64,128]{1,0:T(8,128)},...) custom-call(bf16[64,1024]{1,0:T(8,128)(2,1)S(1)} %get-tuple-element., ...), custom_call_target="tpu_custom_call" | custom-call | tf_op jit(solution)/shard_map/unpack/pallas_call | solution.py:629

commit v4 on v3

--- a/solution.py
+++ b/solution.py
@@ -13,7 +13,7 @@
 BF = jnp.bfloat16
 F32 = jnp.float32
 LOW = 256
-PIECE = 16
+PIECE = 8
 
 
 def nn(a, b):
@@ -43,12 +43,19 @@
     )
 
 
-def lively_and_slope(linear):
-    half = 0.5 * linear
+def lively_and_slope(half):
     tilt = jnp.tanh(half)
-    logistic = 0.5 + 0.5 * tilt
-    lively = half + half * tilt
-    return lively, logistic + lively * (1.0 - logistic)
+    tilted = half * tilt
+    return half + tilted, (1.0 + tilt) + (half - tilted * tilt)
+
+
+def pipeline(number, lag, stages):
+    values = [None] * number
+    for t in range(number + lag * (len(stages) - 1)):
+        for k in reversed(range(len(stages))):
+            c = t - k * lag
+            if 0 <= c < number:
+                values[c] = stages[k](c, values[c])
 
 
 def fold_lanes(values):
@@ -72,11 +79,13 @@
         selector[begin : begin + 16, at] = jnp.where(offset == jnp.asarray(begin, BF), one, zero)
 
 
-def choose(stacked, high, first, base):
-    features = base.shape[0]
+def choose(stacked, features, high, first, base=None):
+    blocks = [stacked[i : i + features] for i in range(0, stacked.shape[0], features)]
+    if base is None:
+        base, blocks, first = blocks[0], blocks[1:], first + 1
     high = jnp.broadcast_to(high, base.shape)
-    for i in range(stacked.shape[0] // features):
-        base = jnp.where(high == first + i, stacked[i * features : (i + 1) * features], base)
+    for i, block in enumerate(blocks):
+        base = jnp.where(high == first + i, block, base)
     return base
 
 
@@ -84,6 +93,19 @@
     high = jnp.concatenate([high] * (values.shape[0] // 16), axis=0)
     zero = jnp.zeros(values.shape, values.dtype)
     return jnp.concatenate([jnp.where(high == jnp.asarray(i, BF), values, zero) for i in blocks], axis=0)
+
+
+def split_products(chunks, groups):
+    totals = [None] * len(groups)
+    for values, high, turned in chunks:
+        for g, blocks in enumerate(groups):
+            part = nn(spread_blocks(values, high, blocks), turned)
+            totals[g] = part if totals[g] is None else totals[g] + part
+    return jnp.concatenate(totals, axis=0)
+
+
+def halves_of(first, number):
+    return range(first, first + number // 2), range(first + number // 2, first + number)
 
 
 def high_part(index):
@@ -190,11 +212,15 @@
 
 
 def edge_owner(count, j):
-    return count // 2 - 4 + j
+    return 2 * j + 1
 
 
 def node_owner(count, j):
-    return count // 2 + (j - 8 if j < 4 else j)
+    return count // 2 - 8 + j
+
+
+def vector_owner(count, j):
+    return count // 2 - 1
 
 
 class Reduction:
@@ -231,7 +257,7 @@
             self.result[self.mine] = total.astype(BF)
 
             def body(k):
-                rank = lax.rem(self.me + 1 + lax.rem(k + self.count // 2, self.count - 1), self.count)
+                rank = k + jnp.where(k >= self.me, 1, 0)
                 pltpu.make_async_remote_copy(
                     src_ref=self.reduced,
                     dst_ref=self.result.at[self.mine],
@@ -246,9 +272,10 @@
     def settle(self):
         @pl.when(self.is_owner)
         def _():
-            await_bytes(self.packed.at[pl.ds(0, self.number - 1)], self.sems.at[0])
+            if self.number > 1:
+                await_bytes(self.packed.at[pl.ds(0, self.number - 1)], self.sems.at[0])
+                await_bytes(self.result.at[pl.ds(0, self.number - 1)], self.sems.at[3])
             await_bytes(self.landing, self.sems.at[2])
-            await_bytes(self.result.at[pl.ds(0, self.number - 1)], self.sems.at[3])
 
         @pl.when(jnp.logical_not(self.is_owner))
         def _():
@@ -257,20 +284,21 @@
 
 
 def layer_kernel(
-    dom, sub, chunk,
+    dom, sub,
     node_in, edge_in, senders_in, receivers_in, index_in, node_cot_in, edge_cot_in,
     edge_first_in, edge_second_in, node_first_in, node_second_in,
     edge_bias_in, edge_gain_in, edge_shift_in, node_bias_in, node_gain_in,
-    state_ref, edge_out_ref, edge_sum, node_sum,
+    state_ref, edge_out_ref, edge_sum, node_sum, vector_sum,
     node_ref, edge_ref, senders_ref, receivers_ref, index_ref, node_cot_ref, edge_cot_ref,
     edge_first_ref, edge_second_ref, node_first_ref, node_second_ref,
     edge_bias_ref, edge_gain_ref, edge_shift_ref, node_bias_ref, node_gain_ref,
     outgoing, incoming, returning, returned,
-    export_sel, sender_sel, receiver_sel, sender_high, receiver_high, export_high,
-    stacked, slope, active, scaled_all, spread_all, summed, by_sender, by_receiver, grads, lanes, local,
-    edge_packed, node_packed, edge_landing, node_landing, edge_reduced, node_reduced,
+    export_sel, sender_sel, receiver_sel, sender_turned, receiver_turned, sender_high, receiver_high, export_high,
+    stacked, slope, active, scaled_all, spread_all, lanes, local,
+    edge_packed, node_packed, vector_packed, edge_landing, node_landing, vector_landing,
+    edge_reduced, node_reduced, vector_reduced,
     load_sem, send_sem, recv_sem, back_send, back_recv,
-    edge_sems, node_sems, known,
+    edge_sems, node_sems, vector_sems, known,
 ):
     features, cells = node_ref.shape
     faces = edge_ref.shape[1]
@@ -279,7 +307,6 @@
     own_blocks = cells // LOW
     ghost_blocks = ghosts // LOW
     per = LOW // halo
-    chunks = faces // chunk
     d, s = lax.axis_index("dom"), lax.axis_index("sub")
     count = dom * sub
     me = d * sub + s
@@ -307,9 +334,6 @@
     loads[0].wait()
     loads[1].wait()
 
-    def halves(i):
-        return pl.ds(pl.multiple_of(i * LOW, LOW), LOW)
-
     table = stack_blocks(node_ref[...])
 
     def pick(i):
@@ -317,7 +341,7 @@
         index = index_ref[:, here]
         write_selector(export_sel, here, index)
         export_high[:, here] = high_rows(index)
-        picked = choose(nn(table, export_sel[:, here]), high_part(index), 0, jnp.zeros((features, LOW), F32))
+        picked = choose(nn(table, export_sel[:, here]), features, high_part(index), 0, jnp.zeros((features, LOW), F32))
         picked = picked.astype(BF)
         for p in range(per):
             outgoing[i * per + p] = picked[:, p * halo : (p + 1) * halo]
@@ -337,32 +361,39 @@
         load.wait()
     edge_first_t = edge_first_ref[...]
     edge_first = flip(edge_first_t).astype(BF)
+    edge_half_t = edge_first_t * jnp.asarray(0.5, BF)
     edge_second = edge_second_ref[...]
     edge_second_t = flip(edge_second).astype(BF)
+    edge_second_half = edge_second * jnp.asarray(0.5, BF)
     vectors = [edge_bias_ref, edge_gain_ref, edge_shift_ref, node_bias_ref, node_gain_ref]
     columns = jnp.concatenate([v[...] for v in vectors] + [jnp.zeros((3, features), F32)], axis=0).T
     edge_bias, edge_gain, edge_shift, node_bias, node_gain = (columns[:, i : i + 1] for i in range(5))
 
-    def span(c):
-        return pl.ds(pl.multiple_of(c * chunk, chunk), chunk)
-
-    everything = pl.ds(0, faces)
-
-    def prepare(here):
+    step = math.gcd(faces, 512)
+    steps = faces // step
+
+    def block(c):
+        return pl.ds(c * step, step)
+
+    def gather_own(c, _):
+        here = block(c)
         sender = senders_ref[:, here]
         receiver = receivers_ref[:, here]
+        write_selector(receiver_sel, here, receiver)
+        receiver_high[:, here] = high_rows(receiver)
+        received = choose(nn(table, receiver_sel[:, here]), features, high_part(receiver), 0).astype(BF)
+        stacked[features:, here] = received
         write_selector(sender_sel, here, sender)
-        write_selector(receiver_sel, here, receiver)
         sender_high[:, here] = high_rows(sender)
-        receiver_high[:, here] = high_rows(receiver)
-        zero = jnp.zeros((features, faces), F32)
-        received = choose(nn(table, receiver_sel[:, here]), high_part(receiver), 0, zero).astype(BF)
-        sent = choose(nn(table, sender_sel[:, here]), high_part(sender), 0, zero).astype(BF)
-        stacked[:features, here] = sent
-        stacked[features:, here] = received
-        slope[:, here] = nn(edge_first_t[:, features:], jnp.concatenate([received, edge_ref[:, here]], axis=0)) + edge_bias
-
-    prepare(everything)
+        stacked[:features, here] = choose(nn(table, sender_sel[:, here]), features, high_part(sender), 0).astype(BF)
+        return received
+
+    def first_half(c, received):
+        here = block(c)
+        stack = jnp.concatenate([received, edge_ref[:, here]], axis=0)
+        slope[:, here] = nn(edge_half_t[:, features:], stack) + 0.5 * edge_bias
+
+    pipeline(steps, 1, (gather_own, first_half))
     for (level, reach), (after, further) in zip(levels[:1], levels[1:2]):
         hear(dom, known, level, reach)
         announce(dom, known, after, further)
@@ -373,36 +404,62 @@
 
         return jnp.concatenate([block(i) for i in range(o * third, (o + 1) * third)], axis=0)
 
-    def gather_ghosts(o):
+    def gather_ghosts(o, here):
+        high = high_part(senders_ref[:, here])
+        base = stacked[:features, here].astype(F32)
+        sent = choose(nn(ghost_tables[o], sender_sel[:, here]), features, high, own_blocks + o * third, base).astype(BF)
+        stacked[:features, here] = sent
+        return sent
+
+    for c in range(steps):
+        receiver_turned[block(c)] = receiver_sel[:, block(c)].T
+        sender_turned[block(c)] = sender_sel[:, block(c)].T
+    ghost_tables = {}
+    for o in (1, 2):
         settle_exchange(dom, sub, incoming, recv_sem, False, (o,))
-        high = high_part(senders_ref[...])
-        base = stacked[:features].astype(F32)
-        return choose(nn(ghosts_of(o), sender_sel[...]), high, own_blocks + o * third, base).astype(BF)
-
-    for o in (1, 0):
-        stacked[:features] = gather_ghosts(o)
-    settle_exchange(dom, sub, incoming, recv_sem, False, (2,))
+        ghost_tables[o] = ghosts_of(o)
+        for c in range(steps):
+            gather_ghosts(o, block(c))
+    settle_exchange(dom, sub, incoming, recv_sem, False, (0,))
     for (level, reach), (after, further) in zip(levels[1:], levels[2:]):
         hear(dom, known, level, reach)
         announce(dom, known, after, further)
-
-    def forward(here):
-        high = high_part(senders_ref[:, here])
-        base = stacked[:features, here].astype(F32)
-        sent = choose(nn(ghosts_of(2), sender_sel[:, here]), high, own_blocks + 2 * third, base).astype(BF)
-        stacked[:features, here] = sent
-        lively, steep = lively_and_slope(nn(edge_first_t[:, :features], sent) + slope[:, here])
+    ghost_tables[0] = ghosts_of(0)
+
+    forward_step = math.gcd(faces, 256)
+
+    def forward_block(c):
+        return pl.ds(c * forward_step, forward_step)
+
+    def gather_last(c, _):
+        return gather_ghosts(0, forward_block(c))
+
+    def first_layer(c, sent):
+        here = forward_block(c)
+        lively, steep = lively_and_slope(nn(edge_half_t[:, :features], sent) + slope[:, here])
         lively = lively.astype(BF)
         slope[:, here] = steep
         active[:, here] = lively
+        return lively
+
+    def second_layer(c, lively):
+        here = forward_block(c)
         scaled, spread = standardize(nn(edge_second_t, lively))
         scaled_all[:, here] = scaled
         spread_all[:, here] = spread
         message = (scaled * edge_gain + edge_shift).astype(BF)
-        message = spread_blocks(message, receiver_high[:, here], range(own_blocks))
-        summed[...] = nt(message, receiver_sel[:, here])
-
-    forward(everything)
+        return message
+
+    sums = [None, None]
+
+    def add_messages(c, message):
+        here = forward_block(c)
+        for g, blocks in enumerate(halves_of(0, own_blocks)):
+            part = nn(spread_blocks(message, receiver_high[:, here], blocks), receiver_turned[here])
+            sums[g] = part if sums[g] is None else sums[g] + part
+
+    pipeline(faces // forward_step, 3, (gather_last, first_layer, second_layer, add_messages))
+    summed = jnp.concatenate(sums, axis=0)
 
     def unstack(values):
         return jnp.concatenate([values[i : i + features] for i in range(0, values.shape[0], features)], axis=1)
@@ -410,13 +467,13 @@
     node_first_t = node_first_ref[...]
     node_first = flip(node_first_t).astype(BF)
     node_second_t = flip(node_second_ref[...]).astype(BF)
-    node_input = jnp.concatenate([node_ref[...], unstack(summed[...]).astype(BF)], axis=0)
-    node_lively, node_slope = lively_and_slope(nn(node_first_t, node_input) + node_bias)
+    node_input = jnp.concatenate([node_ref[...], unstack(summed).astype(BF)], axis=0)
+    node_lively, node_slope = lively_and_slope(0.5 * (nn(node_first_t, node_input) + node_bias))
     node_active = node_lively.astype(BF)
     node_scaled, node_spread = standardize(nn(node_second_t, node_active))
     upstream = node_cot_ref[...].astype(F32)
     node_delta = normalize_back(upstream, node_scaled, node_spread, node_gain).astype(BF)
-    node_hidden = nn(node_second_ref[...], node_delta) * node_slope
+    node_hidden = nn(node_second_ref[...], node_delta) * (0.5 * node_slope)
     lanes[3] = fold_lanes(upstream * node_scaled)
     lanes[4] = fold_lanes(upstream)
     lanes[5] = fold_lanes(node_hidden)
@@ -436,16 +493,17 @@
         for j in range(values.shape[0] // PIECE):
             packed[begin + j] = values[j * PIECE : (j + 1) * PIECE].astype(BF)
 
-    edge_number = edge_packed.shape[0]
-    half = count // 2
-    edge_mine = me - edge_owner(count, 0)
     edge_reduction = Reduction(
-        count, sub, me, edge_owner, (edge_mine >= 0) & (edge_mine < edge_number), edge_mine,
+        count, sub, me, edge_owner, (me < 32) & (lax.rem(me, 2) == 1), me // 2,
         edge_packed, edge_landing, edge_reduced, edge_sum, edge_sems,
     )
     node_reduction = Reduction(
-        count, sub, me, node_owner, ((me >= half - 8) & (me < half - 4)) | ((me >= half + 4) & (me < half + 8)),
-        jnp.where(me < half, me - half + 8, me - half), node_packed, node_landing, node_reduced, node_sum, node_sems,
+        count, sub, me, node_owner, (me >= count // 2 - 8) & (me < count // 2 + 8), me - (count // 2 - 8),
+        node_packed, node_landing, node_reduced, node_sum, node_sems,
+    )
+    vector_reduction = Reduction(
+        count, sub, me, vector_owner, me == vector_owner(count, 0), 0,
+        vector_packed, vector_landing, vector_reduced, vector_sum, vector_sems,
     )
     pack(node_packed, 0, nt(node_hidden, node_input))
     node_right = jnp.concatenate([nt(node_active, node_delta), columns_of(3)[:, :features]], axis=1)
@@ -455,75 +513,88 @@
     node_reduction.send_parts()
 
 
-    def backward(here):
-        zero = jnp.zeros((features, faces), F32)
-        gathered = nn(toward, receiver_sel[:, here])
-        delta = edge_cot_ref[:, here].astype(F32) + choose(gathered, high_part(receivers_ref[:, here]), 0, zero)
+    backward_step = math.gcd(faces, 3072)
+
+    def backward_block(c):
+        return pl.ds(c * backward_step, backward_step)
+
+    def gather_toward(c, _):
+        here = backward_block(c)
+        return choose(nn(toward, receiver_sel[:, here]), features, high_part(receivers_ref[:, here]), 0)
+
+    folded = []
+
+    def norm_back(c, gathered):
+        here = backward_block(c)
+        delta = edge_cot_ref[:, here].astype(F32) + gathered
         scaled = scaled_all[:, here]
-        lanes[0] = fold_lanes(delta * scaled)
-        lanes[1] = fold_lanes(delta)
-        edge_delta = normalize_back(delta, scaled, spread_all[:, here], edge_gain).astype(BF)
-        grads[:, 192:] = nt(active[:, here], edge_delta)
-        hidden = nn(edge_second, edge_delta) * slope[:, here]
-        lanes[2] = fold_lanes(hidden)
+        folded.append([fold_lanes(delta * scaled), fold_lanes(delta)])
+        return normalize_back(delta, scaled, spread_all[:, here], edge_gain).astype(BF)
+
+    second_grads, first_grads, edge_grads = [], [], []
+
+    def hidden_of(c, edge_delta):
+        here = backward_block(c)
+        hidden = nn(edge_second_half, edge_delta) * slope[:, here]
+        second_grads.append(nt(active[:, here], edge_delta))
+        folded[c].append(fold_lanes(hidden))
         hidden = hidden.astype(BF)
         active[:, here] = hidden
-        grads[:, :128] = nt(hidden, stacked[:, here])
-        grads[:, 128:192] = nt(hidden, edge_ref[:, here])
-
-    backward(everything)
-    pack(edge_packed, 0, grads[:, :128])
-    pack(edge_packed, features // PIECE, grads[:, 128:])
-    edge_packed[edge_number - 1] = jnp.concatenate(
-        [columns_of(0).T[:PIECE], jnp.zeros((PIECE, 128 - features), F32)], axis=1
-    ).astype(BF)
+        return hidden
+
+    def first_grad(c, hidden):
+        here = backward_block(c)
+        first_grads.append(nt(hidden, stacked[:, here]))
+        edge_grads.append(nt(hidden, edge_ref[:, here]))
+
+    pipeline(faces // backward_step, 1, (gather_toward, norm_back, hidden_of, first_grad))
+    for i in range(3):
+        lanes[i] = functools.reduce(jnp.add, [f[i] for f in folded])
+    pack(edge_packed, 0, functools.reduce(jnp.add, first_grads))
+    right = [functools.reduce(jnp.add, edge_grads), functools.reduce(jnp.add, second_grads)]
+    pack(edge_packed, features // PIECE, jnp.concatenate(right, axis=1))
     edge_reduction.send_parts()
-
-    by_sender[...] = jnp.zeros(by_sender.shape, F32)
-    by_receiver[...] = jnp.zeros(by_receiver.shape, F32)
-    ghost_rows = ghost_blocks * features
-
-    def scatter_ghosts(c, carry):
-        here = span(c)
-        values = spread_blocks(active[:, here], sender_high[:, here], range(own_blocks, own_blocks + ghost_blocks))
-        by_sender[:ghost_rows] += nt(values, sender_sel[:, here])
-        return carry
-
-    lax.fori_loop(0, chunks, scatter_ghosts, 0)
+    vector_packed[0] = jnp.concatenate([columns_of(0).T[:PIECE], jnp.zeros((PIECE, 128 - features), F32)], axis=1).astype(BF)
+    vector_reduction.send_parts()
+
+    wide = math.gcd(faces, 1024)
+
+    def pieces(turned, high):
+        spans = [pl.ds(c * wide, wide) for c in range(faces // wide)]
+        return [(active[:, here], high[:, here], turned[here]) for here in spans]
+
+    by_ghost = split_products(pieces(sender_turned, sender_high), halves_of(own_blocks, ghost_blocks)).astype(BF)
     for i in range(ghost_blocks):
-        back = nn(edge_first[:features], by_sender[i * features : (i + 1) * features].astype(BF)).astype(BF)
+        back = nn(edge_first[:features], by_ghost[i * features : (i + 1) * features]).astype(BF)
         for p in range(per):
             returning[i * per + p] = back[:, p * halo : (p + 1) * halo]
     start_exchange(dom, sub, s, returning, returned, back_send, back_recv, forward=False)
-
-    def scatter_own(c, carry):
-        here = span(c)
-        hidden = active[:, here]
-        by_sender[ghost_rows:] += nt(spread_blocks(hidden, sender_high[:, here], range(own_blocks)), sender_sel[:, here])
-        by_receiver[...] += nt(spread_blocks(hidden, receiver_high[:, here], range(own_blocks)), receiver_sel[:, here])
-        ahead = nn(edge_first[2 * features :], hidden)
+    by_sender = split_products(pieces(sender_turned, sender_high), halves_of(0, own_blocks))
+    by_receiver = split_products(pieces(receiver_turned, receiver_high), halves_of(0, own_blocks))
+    node_reduction.reduce()
+    for c in range(steps):
+        here = block(c)
+        ahead = nn(edge_first[2 * features :], active[:, here])
         edge_out_ref[:, here] = (edge_cot_ref[:, here].astype(F32) + ahead).astype(BF)
-        return carry
-
-    lax.fori_loop(0, chunks, scatter_own, 0)
-    both = jnp.concatenate([unstack(by_sender[ghost_rows:]), unstack(by_receiver[...])], axis=0).astype(BF)
+    both = jnp.concatenate([unstack(by_sender), unstack(by_receiver)], axis=0).astype(BF)
     weights = jnp.concatenate([edge_first[:features], edge_first[features : 2 * features]], axis=1)
     local[...] += nn(weights, both)
 
-    node_reduction.reduce()
     edge_reduction.reduce()
+    vector_reduction.reduce()
     settle_exchange(dom, sub, returned, back_recv, True)
     exported = jnp.concatenate([returned[k] for k in range(peers)], axis=1)
-    exported = spread_blocks(exported, export_high[...], range(own_blocks))
-    state_ref[...] = (local[...] + unstack(nt(exported, export_sel[...]))).astype(BF)
+    arrived = [nt(spread_blocks(exported, export_high[...], g), export_sel[...]) for g in (range(own_blocks),)]
+    state_ref[...] = (local[...] + unstack(jnp.concatenate(arrived, axis=0))).astype(BF)
     settle_exchange(dom, sub, outgoing, send_sem, True)
     settle_exchange(dom, sub, returning, back_send, False)
     node_reduction.settle()
     edge_reduction.settle()
+    vector_reduction.settle()
 
 
 def unpack_kernel(
-    factor, state_in, edge_in, edge_sum, node_sum,
+    factor, state_in, edge_in, edge_sum, node_sum, vector_sum,
     state_ref, edge_ref, edge_first_ref, edge_second_ref, node_first_ref, node_second_ref,
     edge_gain_ref, edge_shift_ref, edge_bias_ref, node_gain_ref, node_shift_ref, node_bias_ref,
 ):
@@ -539,7 +610,7 @@
     edge_first_ref[:, : 2 * features] = block(edge_sum, 0)
     edge_first_ref[:, 2 * features :] = right[:, :features]
     edge_second_ref[...] = right[:, features:]
-    edge_vectors = edge_sum[2 * pieces].astype(F32) * factor
+    edge_vectors = vector_sum[0].astype(F32) * factor
     node_first_ref[...] = block(node_sum, 0)
     right = block(node_sum, pieces)
     node_second_ref[...] = right[:, :features]
@@ -561,9 +632,7 @@
     peers = 3 * sub
     ghosts = peers * halo
     count = dom * sub
-    chunk = math.gcd(faces, 1536)
-    edge_number = 2 * features // PIECE + 1
-    node_number = 2 * features // PIECE
+    number = 2 * features // PIECE
     vmem = pl.BlockSpec(memory_space=pltpu.VMEM)
     hbm = pl.BlockSpec(memory_space=pltpu.HBM)
     shape = jax.ShapeDtypeStruct
@@ -577,24 +646,25 @@
         node_cotangent, edge_cotangent, edge_first.T, edge_second, node_first.T, node_second,
         line(edge_bias), line(edge_gain), line(edge_shift), line(node_bias), line(node_gain),
     )
-    own_rows = cells // LOW * features
-    ghost_rows = ghosts // LOW * features
-    state, edge_result, edge_total, node_total = pl.pallas_call(
-        functools.partial(layer_kernel, dom, sub, chunk),
+    state, edge_result, *totals = pl.pallas_call(
+        functools.partial(layer_kernel, dom, sub),
         out_shape=(
             shape((features, cells), BF),
             shape((features, faces), BF),
-            shape((edge_number, PIECE, 128), BF),
-            shape((node_number, PIECE, 128), BF),
+            shape((number, PIECE, 128), BF),
+            shape((number, PIECE, 128), BF),
+            shape((1, PIECE, 128), BF),
         ),
         in_specs=[hbm] * 16,
-        out_specs=(vmem,) * 4,
+        out_specs=(vmem,) * 5,
         scratch_shapes=[pltpu.VMEM(x.shape, x.dtype) for x in operands]
         + [pltpu.VMEM((peers, features, halo), BF)] * 4
         + [
             pltpu.VMEM((LOW, ghosts), BF),
             pltpu.VMEM((LOW, faces), BF),
             pltpu.VMEM((LOW, faces), BF),
+            pltpu.VMEM((faces, LOW), BF),
+            pltpu.VMEM((faces, LOW), BF),
             pltpu.VMEM((16, faces), BF),
             pltpu.VMEM((16, faces), BF),
             pltpu.VMEM((16, ghosts), BF),
@@ -603,22 +673,17 @@
             pltpu.VMEM((features, faces), BF),
             pltpu.VMEM((features, faces), F32),
             pltpu.VMEM((1, faces), F32),
-            pltpu.VMEM((own_rows, LOW), F32),
-            pltpu.VMEM((ghost_rows + own_rows, LOW), F32),
-            pltpu.VMEM((own_rows, LOW), F32),
-            pltpu.VMEM((features, 4 * features), F32),
             pltpu.VMEM((6, features, 128), F32),
             pltpu.VMEM((features, cells), F32),
-            pltpu.VMEM((edge_number, PIECE, 128), BF),
-            pltpu.VMEM((node_number, PIECE, 128), BF),
-            pltpu.VMEM((count - 1, PIECE, 128), BF),
-            pltpu.VMEM((count - 1, PIECE, 128), BF),
-            pltpu.VMEM((PIECE, 128), BF),
-            pltpu.VMEM((PIECE, 128), BF),
+            pltpu.VMEM((number, PIECE, 128), BF),
+            pltpu.VMEM((number, PIECE, 128), BF),
+            pltpu.VMEM((1, PIECE, 128), BF),
         ]
+        + [pltpu.VMEM((count - 1, PIECE, 128), BF)] * 3
+        + [pltpu.VMEM((PIECE, 128), BF)] * 3
         + [dma((16,))]
         + [dma((3,))] * 4
-        + [dma((4,))] * 2
+        + [dma((4,))] * 3
         + [pltpu.SemaphoreType.REGULAR((max(1, len(list(reaches(dom)))),))],
         compiler_params=pltpu.CompilerParams(
             collective_id=0, has_side_effects=True, vmem_limit_bytes=32 * 1024 * 1024
@@ -637,11 +702,11 @@
             shape(node_second.shape, F32),
         )
         + (vector,) * 6,
-        in_specs=[vmem] * 4,
+        in_specs=[vmem] * 5,
         out_specs=(vmem,) * 12,
         compiler_params=pltpu.CompilerParams(vmem_limit_bytes=16 * 1024 * 1024),
         name="unpack",
-    )(state, edge_result, edge_total, node_total)
+    )(state, edge_result, *totals)
     state, edge_result, edge_first_sum, edge_second_sum, node_first_sum, node_second_sum, *vectors = results
     vectors = [v.reshape(-1) for v in vectors]
     return (

time: 26.6 us -> 23.8 us (0.89)
  Pallas kernels: 25.8 us -> 23 us
    pallas_call x1, Pallas kernels: 24.9 us -> 22.1 us  [on_device(): pl.pallas_call(functools.partial(layer_kernel, dom, sub), out_shape=(shap...]
where the time goes in v4:
time: 23.8 us; the launch traced here: 23.6 us
  Pallas kernels  23 us (97%)
  between operations  0.66 us (3%)
    pallas_call x1, Pallas kernels, on_device(): pl.pallas_call(functools.partial(layer_kernel, dom, sub), out_shape=(shap...  22.1 us
    pallas_call x1, Pallas kernels, on_device(): pl.pallas_call(functools.partial(unpack_kernel, 1.0 / math.sqrt(faces * c...  0.88 us

profile of v4, /device:TPU:0, one launch (start us, length us, event | category | flops | bytes accessed | tf_op | source)
XLA Modules:
  0.0 23.6 jit_solution(3889998294225052444)
XLA Ops:
  0.7 22.1 %layer.1 = (bf16[64,1024]{1,0:T(8,128)(2,1)S(1)}, bf16[64,3072]{1,0:T(8,128)(2,1)S(1)}, bf16[16,8,128]{2,1,0:T(8,128)(2,1)S(1)}, bf16[16,8,128]{2,1,0:T(8,128)(2,1)S(1)}, bf16[1,8,128]{2,1,0:T(8,128)(2,1)S(1)}) custom-call(bf16[64,1024]{1,0:T(8,128)(2,1)} %node_in.1, bf16[64,3072]{1,0:T(8,128)(2,1)} %edge_in.1, s32[1,3072]{1,0:T(1,128)} %bitcast.20, ...), custom_call_target="tpu_custom_call" | custom-call | tf_op jit(solution)/shard_map/layer/pallas_call | solution.py:649
  22.7 0.9 %unpack.1 = (bf16[64,1024]{1,0:T(8,128)(2,1)}, bf16[64,3072]{1,0:T(8,128)(2,1)}, f32[64,192]{1,0:T(8,128)}, f32[64,64]{1,0:T(8,128)}, f32[64,128]{1,0:T(8,128)},...) custom-call(bf16[64,1024]{1,0:T(8,128)(2,1)S(1)} %get-tuple-element., ...), custom_call_target="tpu_custom_call" | custom-call | tf_op jit(solution)/shard_map/unpack/pallas_call | solution.py:694

commit v5 on v4

--- a/solution.py
+++ b/solution.py
@@ -209,14 +209,6 @@
             await_bytes(blocks.at[pl.ds(o * sub, number)], sem.at[o])
 
         guarded(o, (row >= 0) & (row < dom), finish)
-
-
-def edge_owner(count, j):
-    return 2 * j + 1
-
-
-def node_owner(count, j):
-    return count // 2 - 8 + j
 
 
 def vector_owner(count, j):
@@ -493,12 +485,21 @@
         for j in range(values.shape[0] // PIECE):
             packed[begin + j] = values[j * PIECE : (j + 1) * PIECE].astype(BF)
 
+    number = edge_packed.shape[0]
+
+    def edge_owner(count, j):
+        return 2 * (number - j) - 1
+
+    def node_owner(count, j):
+        return count // 2 - number // 2 + j
+
+    node_mine = me - node_owner(count, 0)
     edge_reduction = Reduction(
-        count, sub, me, edge_owner, (me < 32) & (lax.rem(me, 2) == 1), me // 2,
+        count, sub, me, edge_owner, (me < 2 * number) & (lax.rem(me, 2) == 1), number - 1 - me // 2,
         edge_packed, edge_landing, edge_reduced, edge_sum, edge_sems,
     )
     node_reduction = Reduction(
-        count, sub, me, node_owner, (me >= count // 2 - 8) & (me < count // 2 + 8), me - (count // 2 - 8),
+        count, sub, me, node_owner, (node_mine >= 0) & (node_mine < number), node_mine,
         node_packed, node_landing, node_reduced, node_sum, node_sems,
     )
     vector_reduction = Reduction(

time: 23.8 us -> 23.6 us (level)
  no operation moved by 1% of the time
where the time goes in v5:
time: 23.6 us; the launch traced here: 23.4 us
  Pallas kernels  22.8 us (97%)
  between operations  0.66 us (3%)
    pallas_call x1, Pallas kernels, on_device(): pl.pallas_call(functools.partial(layer_kernel, dom, sub), out_shape=(shap...  21.9 us
    pallas_call x1, Pallas kernels, on_device(): pl.pallas_call(functools.partial(unpack_kernel, 1.0 / math.sqrt(faces * c...  0.88 us

profile of v5, /device:TPU:0, one launch (start us, length us, event | category | flops | bytes accessed | tf_op | source)
XLA Modules:
  0.0 23.4 jit_solution(14009684886650915140)
XLA Ops:
  0.7 21.9 %layer.1 = (bf16[64,1024]{1,0:T(8,128)(2,1)S(1)}, bf16[64,3072]{1,0:T(8,128)(2,1)S(1)}, bf16[16,8,128]{2,1,0:T(8,128)(2,1)S(1)}, bf16[16,8,128]{2,1,0:T(8,128)(2,1)S(1)}, bf16[1,8,128]{2,1,0:T(8,128)(2,1)S(1)}) custom-call(bf16[64,1024]{1,0:T(8,128)(2,1)} %node_in.1, bf16[64,3072]{1,0:T(8,128)(2,1)} %edge_in.1, s32[1,3072]{1,0:T(1,128)} %bitcast.20, ...), custom_call_target="tpu_custom_call" | custom-call | tf_op jit(solution)/shard_map/layer/pallas_call | solution.py:650
  22.5 0.9 %unpack.1 = (bf16[64,1024]{1,0:T(8,128)(2,1)}, bf16[64,3072]{1,0:T(8,128)(2,1)}, f32[64,192]{1,0:T(8,128)}, f32[64,64]{1,0:T(8,128)}, f32[64,128]{1,0:T(8,128)},...) custom-call(bf16[64,1024]{1,0:T(8,128)(2,1)S(1)} %get-tuple-element., ...), custom_call_target="tpu_custom_call" | custom-call | tf_op jit(solution)/shard_map/unpack/pallas_call | solution.py:695
